TPU v7x, 128 devices: a whole 4x4x4 slice. The times are simulated.
128 devices in a mesh: dp: 1, dcp: 128 (over z, y, x, core).
Axes of the slice: x: 4, y: 4, z: 4, core: 2. Of those that a mesh axis runs over, the one named last changes fastest.
Arguments:
- q: bfloat16 [32, 128, 576], P('dp', 'dcp')
- cache: bfloat16 [32, 32, 128, 8, 576], P('dp', None, 'dcp')
- lens: int32 [32], P('dp')
Outputs:
- output: bfloat16 [32, 128, 512], P('dp', 'dcp')
All inputs are finite; a program needn't handle non-finite values.
Results may differ from a plain program's by a relative error of at most 0.00544788.
Values are sent between devices in bfloat16 or wider.
A program may use at most 1 GiB of HBM per device.

v0:
```python
import jax
import jax.numpy as jnp
from jax import lax
from jax.sharding import PartitionSpec as P

ROPE = 64
QK_DIM = 192
SCALE = QK_DIM ** -0.5


def solution(mesh):
    n = mesh.shape['dcp']

    def local(q, cache, lens):
        b, hl, k = q.shape
        r = cache.shape[1]
        page = cache.shape[3]
        lorav = k - ROPE
        d = lax.axis_index('dcp')
        qa = lax.all_gather(q, 'dcp', axis=1, tiled=True)
        c = cache.reshape(b, r * page, k)
        pos = (jnp.arange(r)[:, None] * n + d) * page + jnp.arange(page)[None, :]
        valid = pos.reshape(r * page)[None, :] < lens[:, None]
        s = jnp.einsum('bhk,btk->bht', qa, c, preferred_element_type=jnp.float32) * SCALE
        s = jnp.where(valid[:, None, :], s, -jnp.inf)
        m = jnp.max(s, axis=2)
        m = jnp.where(jnp.isfinite(m), m, 0.0)
        p = jnp.exp(s - m[:, :, None])
        l = jnp.sum(p, axis=2)
        has = l > 0.0
        lsafe = jnp.where(has, l, 1.0)
        pv = jnp.einsum('bht,btk->bhk', p.astype(jnp.bfloat16), c[:, :, :lorav], preferred_element_type=jnp.float32)
        od = (pv / lsafe[:, :, None]).astype(jnp.bfloat16)
        lse = jnp.where(has, m + jnp.log(lsafe), -jnp.inf)
        od = lax.all_to_all(od.reshape(b, n, hl, lorav), 'dcp', 1, 1, tiled=True)
        lse = lax.all_to_all(lse.reshape(b, n, hl), 'dcp', 1, 1, tiled=True)
        top = jnp.max(lse, axis=1)
        w = jnp.exp(lse - top[:, None, :])
        o = jnp.sum(w[:, :, :, None] * od.astype(jnp.float32), axis=1) / jnp.sum(w, axis=1)[:, :, None]
        return o.astype(jnp.bfloat16)

    return jax.shard_map(local, mesh=mesh, in_specs=(P('dp', 'dcp', None), P('dp', None, 'dcp', None, None), P('dp')), out_specs=P('dp', 'dcp', None), check_vma=False)
```

profile of v0, /device:TPU:1, one launch (start us, length us, event | category | flops | bytes accessed | tf_op | source)
XLA Modules:
  0.0 191.4 jit_solution(11599062554165926348)
XLA Ops:
  6.5 0.0 all-gather.2.cloned.1.call-start
  6.5 0.7 all-gather.2.cloned.1.call-update
  7.3 0.1 iota_add_fusion
  7.3 0.1 add.46
  7.4 0.7 broadcast_compare_fusion
  8.2 73.4 %all-gather.2.cloned.1.call-done = bf16[32,128,576]{2,0,1:T(8,128)(2,1)} async-done(((bf16[32,1,576]{2,0,1:T(8,128)(2,1)}), bf16[32,128,576]{2,0,1:T(8,128)(2,1)}) %all-gather.2.cloned.1.call-update) | async-done | bytes 4718608 | tf_op jit(solution)/shard_map/all_gather | solution.py:20
  81.5 11.0 %fusion.5 = (f32[32,128]{1,0:T(8,128)S(1)}, f32[32,128,256]{2,1,0:T(8,128)}) fusion(pred[32,256]{1,0:T(8,128)(4,1)S(1)} %broadcast_compare_fusion, bf16[32,32,1,8,576]{4,3,2,1,0:T(8,128)(2,1)} %param.4, bf16[32,128,576]{2,0,1:T(8,128)(2,1)} %all-gather.2.cloned.1.call-done), kind=kOutput, calls=%fused_computation.9 | convolution fusion | flops 1211101184 | bytes 18374656 | tf_op jit(solution)/shard_map/bhk,btk->bht/dot_general | solution.py:24
  92.6 3.4 %fusion.7 = f32[32,128]{1,0:T(8,128)S(1)} fusion(f32[32,128,256]{2,1,0:T(8,128)} %get-tuple-element.8, f32[32,128]{1,0:T(8,128)S(1)} %is-finite_select_fusion.1, pred[32,256]{1,0:T(8,128)(4,1)S(1)} %broadcast_compare_fusion), kind=kLoop, calls=%fused_computation.11 | loop fusion | flops 4190208 | bytes 4235264 | tf_op jit(solution)/shard_map/reduce_sum | solution.py:29
  96.0 0.7 copy.15
  96.7 5.5 %all-to-all-start = ((f32[32,128,1]{0,2,1:T(1,128)}), f32[32,128,1]{0,2,1:T(1,128)S(1)}, u32[]{:S(2)}, u32[]{:S(2)}) async-start(f32[32,128,1]{0,2,1:T(1,128)} %copy.15), calls=%async_computation | async-start | bytes 131072 | tf_op jit(solution)/shard_map/all_to_all | solution.py:36
  102.2 5.8 %fusion.4 = bf16[32,128,1,512]{3,1,0,2:T(8,128)(2,1)S(1)} fusion(f32[32,128]{1,0:T(8,128)S(1)} %compare_select_fusion, bf16[32,256,576]{2,1,0:T(8,128)(2,1)} %bitcast.17, f32[32,128,256]{2,1,0:T(8,128)} %get-tuple-element.8, f32[32,128]{1,0:T(8,128)S(1)} %is-finite_select_fusion.1, pred[32,256]{1,0:T(8,128)(4,1)S(1)} %broadcast_compare_fusion), kind=kOutput, calls=%fused_computation.8 | convolution fusion | flops 1082130432 | bytes 16818176 | tf_op jit(solution)/shard_map/bht,btk->bhk/dot_general | solution.py:32
  108.0 4.3 %copy.16 = bf16[32,128,1,512]{3,0,2,1:T(8,128)(2,1)} copy(bf16[32,128,1,512]{3,1,0,2:T(8,128)(2,1)S(1)} %fusion.4) | data formatting | bytes 8388608 | tf_op jit(solution)/shard_map/reshape | solution.py:35
  112.3 0.0 all-to-all-done
  112.3 10.2 %all-to-all-start.1 = ((bf16[32,128,1,512]{3,0,2,1:T(8,128)(2,1)}), bf16[32,128,1,512]{3,0,2,1:T(8,128)(2,1)}, u32[]{:S(2)}, u32[]{:S(2)}) async-start(bf16[32,128,1,512]{3,0,2,1:T(8,128)(2,1)} %copy.16), calls=%async_computation.1 | async-start | bytes 8388608 | tf_op jit(solution)/shard_map/all_to_all | solution.py:35
  122.5 0.2 reduce_max.22
  122.7 0.2 fusion.23
  122.9 58.3 %all-to-all-done.1 = bf16[32,128,1,512]{3,0,2,1:T(8,128)(2,1)} async-done(((bf16[32,128,1,512]{3,0,2,1:T(8,128)(2,1)}), bf16[32,128,1,512]{3,0,2,1:T(8,128)(2,1)}, u32[]{:S(2)}, u32[]{:S(2)}) %all-to-all-start.1) | async-done | bytes 4194336 | tf_op jit(solution)/shard_map/all_to_all | solution.py:35
  181.2 2.7 %multiply_reduce_fusion = f32[32,512]{1,0:T(8,128)S(1)} fusion(bf16[32,128,1,512]{3,0,2,1:T(8,128)(2,1)} %all-to-all-done.1, f32[32,128]{0,1:T(8,128)S(1)} %bitcast.16), kind=kLoop, calls=%fused_computation.2 | loop fusion | flops 6275072 | bytes 4276224 | tf_op jit(solution)/shard_map/reduce_sum | solution.py:39
  183.9 0.7 fusion.17
  (4 shorter events, 0.0 us)
Async XLA Ops:
  6.5 75.0 %all-gather.2.cloned.1.call-start = ((), (), s32[]{:S(2)}) async-start(), calls=%async_computation.2 | async-start | bytes 5283840 | tf_op jit(solution)/shard_map/all_gather | solution.py:20
  96.7 15.6 %all-to-all-start = ((f32[32,128,1]{0,2,1:T(1,128)}), f32[32,128,1]{0,2,1:T(1,128)S(1)}, u32[]{:S(2)}, u32[]{:S(2)}) async-start(f32[32,128,1]{0,2,1:T(1,128)} %copy.15), calls=%async_computation | async-start | bytes 131072 | tf_op jit(solution)/shard_map/all_to_all | solution.py:36
  112.3 68.9 %all-to-all-start.1 = ((bf16[32,128,1,512]{3,0,2,1:T(8,128)(2,1)}), bf16[32,128,1,512]{3,0,2,1:T(8,128)(2,1)}, u32[]{:S(2)}, u32[]{:S(2)}) async-start(bf16[32,128,1,512]{3,0,2,1:T(8,128)(2,1)} %copy.16), calls=%async_computation.1 | async-start | bytes 8388608 | tf_op jit(solution)/shard_map/all_to_all | solution.py:35
Sparse Core Ops, SparseCore 0:
  10.3 71.1 all-gather.1
where the time goes:
time: 193 us; the launch traced here: 191 us
  waiting for transfers between devices  132 us (68%)
  matrix products  16.9 us (9%)
  starting transfers between devices  15.7 us (8%)
  between operations  13.5 us (7%)
  other arithmetic  7.92 us (4%)
  local copies, waits for them, and re-layouts  5.12 us (3%)
    all_gather x1, waiting for transfers between devices, local(): qa = lax.all_gather(q, 'dcp', axis=1, tiled=True)  73.4 us
    all_to_all x1, waiting for transfers between devices, local(): od = lax.all_to_all(od.reshape(b, n, hl, lorav), 'dcp', 1, 1, tiled=True)  58.3 us
    dot_general x1, matrix products, local(): jnp.einsum('bhk,btk->bht', qa, c, preferred_element_type=jnp.float32)  11 us
    all_to_all x1, starting transfers between devices, local(): od = lax.all_to_all(od.reshape(b, n, hl, lorav), 'dcp', 1, 1, tiled=True)  10.2 us
    dot_general x1, matrix products, local(): jnp.einsum('bht,btk->bhk', p.astype(jnp.bfloat16), c[:, :, :lorav], prefe...  5.83 us
    all_to_all x1, starting transfers between devices, local(): lse = lax.all_to_all(lse.reshape(b, n, hl), 'dcp', 1, 1, tiled=True)  5.45 us
    reshape x1, local copies, waits for them, and re-layouts, local(): od = lax.all_to_all(od.reshape(b, n, hl, lorav), 'dcp', 1, 1, tiled=True)  4.3 us
  transfers between devices with their start and end apart: 3, of which 2 were waited for; matrix products, arithmetic and copies ran while one was open for 6% of the time, Pallas kernels for 0%

commit v1 on v0

v1 whole, which is shorter than its diff:
```python
import functools
import math

import jax
import jax.numpy as jnp
from jax import lax
from jax.experimental import pallas as pl
from jax.experimental.pallas import tpu as pltpu
from jax.sharding import PartitionSpec as P

ROPE = 64
QK_DIM = 192
SCALE2 = QK_DIM ** -0.5 * math.log2(math.e)
NEG = -3.0e38
MESH = pl.DeviceIdType.MESH
F32 = jnp.float32
BF16 = jnp.bfloat16

STRIDE = (2, 8, 32)
ORDERS = ((0, 1, 2), (1, 2, 0), (2, 0, 1))
COUNT = (6, 5, 5)
NI = 6


LAT, QW, LANES = 512, 576, 128
KS, DIRS, RING, RING_OFFS, LINE_OFFS = range(3), range(2), range(4), range(1, 4), range(1, 8)


def _perm(rows, cols, f):
    r = lax.broadcasted_iota(jnp.int32, (rows, cols), 0)
    c = lax.broadcasted_iota(jnp.int32, (rows, cols), 1)
    return f(r, c).astype(F32).astype(BF16)


def _merge_weights(lses):
    top = functools.reduce(jnp.maximum, lses)
    ws = [jnp.exp2(v - top) for v in lses]
    tot = functools.reduce(jnp.add, ws)
    inv = 1.0 / tot
    return [w * inv for w in ws], top + jnp.log2(tot)


def _kernel(lens, q_h, c_h, o_h,
            q_in, s1src, s1buf, q_all, cbuf, obuf, lrow, lcol,
            r1o, r1ol, mrg, mlse, r1d, r1dl, r1m, lse1,
            r2d, r2l, s3src, s3l, r3d, r3l, oout,
            sem_q, sem_c, sem_ps, sem_pr, s1s, s1r, s2s, s2r, s3s, s3r, sfs, sfr,
            a_s, a_r, al_s, al_r, b_s, b_r, bl_s, bl_r, c_s, c_r, cl_s, cl_r,
            e_s, e_r, el_s, el_r, sem_o):
    d = lax.axis_index('dcp')
    core = d % 2
    co = ((d // 2) % 4, (d // 8) % 4, d // 32)

    def at(axis, pos):
        return {'dcp': d + (pos - co[axis]) * STRIDE[axis]}

    def line(axis, j):
        return {'dcp': d + (j // 2 - co[axis]) * STRIDE[axis] + (j % 2 - core)}

    def rcopy(src, dst, ss, rs, dev):
        return pltpu.make_async_remote_copy(src_ref=src, dst_ref=dst, send_sem=ss, recv_sem=rs,
                                            device_id=dev, device_id_type=MESH)

    def wait_bytes(ref, sem):
        pltpu.make_async_copy(ref, ref, sem).wait()

    load_q = pltpu.make_async_copy(q_h, q_in, sem_q)
    load_q.start()

    def local_cache(s):
        return pltpu.make_async_copy(c_h.at[16 * core + s], cbuf.at[s, pl.ds(32 * core, 32)], sem_c.at[s])

    @pl.loop(0, 16)
    def _(s):
        local_cache(s).start()

    bar = pltpu.get_barrier_semaphore()
    partner = {'dcp': d + 1 - 2 * core}
    pl.semaphore_signal(bar, inc=1, device_id=partner, device_id_type=MESH)
    for a in KS:
        for off in RING_OFFS:
            for c2 in DIRS:
                pl.semaphore_signal(bar, inc=1, device_id=line(a, ((co[a] + off) % 4) * 2 + c2), device_id_type=MESH)

    lrow[...] = jnp.zeros_like(lrow)

    load_q.wait()

    def sel(r, c):
        c2, k, i = r // 24, (r // 8) % 3, r % 8
        s = 3 * i + k
        return (c == 16 * c2 + s) & (s < 16)

    qp = jnp.dot(_perm(48, 32, sel), q_in[...], preferred_element_type=F32).astype(BF16)
    s1src[...] = qp.reshape(2, 3, 8, QW)
    pl.semaphore_wait(bar, 19)

    for k in KS:
        a1 = ORDERS[k][0]
        j0 = co[a1] * 2 + core
        for off in LINE_OFFS:
            j = (j0 + off) % 8
            rcopy(s1src.at[j % 2, k], s1buf.at[k, j0], s1s.at[k, off], s1r.at[k, off], line(a1, j)).start()
        s1buf[k, j0] = s1src[core, k]

    def push_cache(s):
        return rcopy(c_h.at[16 * (1 - core) + s], cbuf.at[s, pl.ds(32 * core, 32)], sem_ps.at[s], sem_pr.at[s], partner)

    def got_cache(s):
        return rcopy(c_h.at[s], cbuf.at[s, pl.ds(32 * (1 - core), 32)], sem_ps.at[s], sem_pr.at[s], partner)

    @pl.loop(0, 16)
    def _(s):
        push_cache(s).start()

    def grp(k, off=0):
        _, a2, a3 = ORDERS[k]
        return co[a3] * 4 + (co[a2] + 4 - off) % 4

    def s2(k, i, off):
        a2 = ORDERS[k][1]
        g = grp(k)
        return rcopy(q_all.at[k, i, g], q_all.at[k, i, g], s2s.at[off - 1], s2r.at[k, i, off - 1],
                     at(a2, (co[a2] + off) % 4))

    def s2_wait(k, i, off):
        g = grp(k, off)
        rcopy(q_all.at[k, i, g], q_all.at[k, i, g], s2s.at[off - 1], s2r.at[k, i, off - 1], partner).wait_recv()

    def s3(k, i, off, dr):
        a3 = ORDERS[k][2]
        g = grp(k, off)
        return rcopy(q_all.at[k, i, g], q_all.at[k, i, g], s3s.at[dr, off], s3r.at[k, i, dr, off],
                     at(a3, (co[a3] + (1 if dr == 0 else 3)) % 4))

    def s3_src(k, off, dr, hops):
        _, a2, a3 = ORDERS[k]
        p3 = (co[a3] + (4 - hops if dr == 0 else hops)) % 4
        return p3 * 4 + (co[a2] + 4 - off) % 4

    def s3_wait(k, i, off, dr):
        g = s3_src(k, off, dr, 1)
        rcopy(q_all.at[k, i, g], q_all.at[k, i, g], s3s.at[dr, off], s3r.at[k, i, dr, off], partner).wait_recv()

    def fwd(k, i, off):
        dr = off // 2
        a3 = ORDERS[k][2]
        g = s3_src(k, off, dr, 1)
        return rcopy(q_all.at[k, i, g], q_all.at[k, i, g], sfs.at[off], sfr.at[k, i, off],
                     at(a3, (co[a3] + (1 if dr == 0 else 3)) % 4))

    def fwd_wait(k, i, off):
        g = s3_src(k, off, off // 2, 2)
        rcopy(q_all.at[k, i, g], q_all.at[k, i, g], sfs.at[off], sfr.at[k, i, off], partner).wait_recv()

    def each(f):
        @pl.loop(0, NI - 1)
        def _(i):
            for k in KS:
                f(k, i)
        f(0, NI - 1)

    tr = _perm(64, 64, lambda r, c: (r // 8 == c % 8) & (r % 8 == c // 8))
    for k in KS:
        a1 = ORDERS[k][0]
        j0 = co[a1] * 2 + core
        for off in LINE_OFFS:
            src = (j0 + 8 - off) % 8
            rcopy(s1src.at[core, k], s1buf.at[k, src], s1s.at[k, off], s1r.at[k, off], partner).wait()
        blk = jnp.dot(tr, s1buf[k].reshape(64, QW), preferred_element_type=F32).astype(BF16).reshape(8, 8, QW)
        g = grp(k)
        for i in range(COUNT[k]):
            q_all[k, i, g] = blk[i]

        @pl.loop(0, COUNT[k])
        def _(i):
            for off in (2, 1, 3):
                s2(k, i, off).start()
            for dr in DIRS:
                s3(k, i, 0, dr).start()

    def stage3(k, i):
        for off in (1, 3, 2):
            s2_wait(k, i, off)
            for dr in DIRS:
                s3(k, i, off, dr).start()

    each(stage3)

    def forward(k, i):
        for off in (0, 1, 3, 2):
            s3_wait(k, i, off, off // 2)
            fwd(k, i, off).start()

    def arrive(k, i):
        s = 3 * i + k
        local_cache(s).wait()
        got_cache(s).wait_recv()
        for off in RING:
            s3_wait(k, i, off, 1 - off // 2)
            fwd_wait(k, i, off)

    chip8 = (d // 2) * 16

    def attend(k, i):
        s = 3 * i + k
        n = lens[16 * core + s]
        cs = cbuf[s].reshape(LAT, QW)
        qs = q_all[k, i].reshape(LANES, QW)
        st = lax.dot_general(cs, qs, (((1,), (1,)), ((), ())), preferred_element_type=F32) * SCALE2
        j = lax.broadcasted_iota(jnp.int32, (LAT, LANES), 0)
        ok = (j & 7) + ((j >> 3) & 31) * 1024 + (j >> 8) * 8 + chip8 < n
        st = jnp.where(ok, st, NEG)
        m = jnp.max(st, axis=0, keepdims=True)
        p = jnp.where(ok, jnp.exp2(st - m), 0.0)
        l = jnp.sum(p, axis=0, keepdims=True)
        has = l > 0.0
        ls = jnp.where(has, l, 1.0)
        pn = (p * (1.0 / ls)).astype(BF16)
        o = lax.dot_general(pn, cs[:, :LAT], (((0,), (0,)), ((), ())), preferred_element_type=F32)
        obuf[k, i] = o.astype(BF16).reshape(16, 8, LAT)
        lrow[k, pl.ds(i, 1), :] = jnp.where(has, m + jnp.log2(ls), NEG)

    def nb(k, dr, hops=1):
        a3 = ORDERS[k][2]
        return (co[a3] + (hops if dr == 0 else 4 - hops)) % 4

    def opp(k, i, dr):
        a3 = ORDERS[k][2]
        return rcopy(obuf.at[k, i, pl.ds(nb(k, 0, 2) * 4 + 2 * dr, 2)], r1o.at[k, i, dr],
                     a_s.at[k, i, dr], a_r.at[k, i, dr], at(a3, nb(k, dr)))

    def plain(k, i, dr):
        a3 = ORDERS[k][2]
        return rcopy(obuf.at[k, i, pl.ds(nb(k, dr) * 4 + 2 * (1 - dr), 2)], r1d.at[k, i, dr, pl.ds(2 * (1 - dr), 2)],
                     b_s.at[k, i, dr, 0], b_r.at[k, i, dr, 0], at(a3, nb(k, dr)))

    def merged(k, i, dr):
        a3 = ORDERS[k][2]
        return rcopy(mrg.at[k, i, dr], r1d.at[k, i, dr, pl.ds(2 * dr, 2)],
                     b_s.at[k, i, dr, 1], b_r.at[k, i, dr, 1], at(a3, nb(k, dr)))

    def send1(k, i):
        for dr in DIRS:
            opp(k, i, dr).start()
        for dr in DIRS:
            plain(k, i, dr).start()

    for k in KS:
        forward(k, 0)
    for k in KS:
        forward(k, 1)

    @pl.loop(0, NI - 1)
    def _(i):
        for k in KS:
            arrive(k, i)
        for k in KS:
            attend(k, i)
        for k in KS:
            send1(k, i)

        @pl.when(i < NI - 3)
        def _():
            for k in KS:
                forward(k, i + 2)

        @pl.when(i == NI - 3)
        def _():
            forward(0, NI - 1)

    arrive(0, NI - 1)
    attend(0, NI - 1)
    send1(0, NI - 1)

    def opp_lse(k, dr):
        a3 = ORDERS[k][2]
        return rcopy(lcol.at[k, pl.ds(nb(k, 0, 2) * 32 + 16 * dr, 16)], r1ol.at[k, dr],
                     al_s.at[k, dr], al_r.at[k, dr], at(a3, nb(k, dr)))

    def dir_lse(k, dr):
        a3 = ORDERS[k][2]
        return rcopy(mlse.at[k, dr], r1dl.at[k, dr], bl_s.at[k, dr], bl_r.at[k, dr], at(a3, nb(k, dr)))

    for k in KS:
        lcol[k] = lrow[k].T
        for dr in DIRS:
            opp_lse(k, dr).start()

    for k in KS:
        for dr in DIRS:
            base = nb(k, dr) * 4
            opp_lse(k, dr).wait_recv()
            mine = lcol[k, pl.ds(base * 8 + 16 * dr, 16), :]
            ws, ml = _merge_weights([mine, r1ol[k, dr]])
            mlse[k, dr, 16 * dr:16 * dr + 16, :] = ml
            mlse[k, dr, 16 * (1 - dr):16 * (1 - dr) + 16, :] = lcol[k, pl.ds(base * 8 + 16 * (1 - dr), 16), :]
            dir_lse(k, dr).start()
            for i in range(COUNT[k]):
                opp(k, i, dr).wait_recv()
                a = obuf[k, i, pl.ds(base + 2 * dr, 2)].reshape(16, LAT).astype(F32)
                b = r1o[k, i, dr].reshape(16, LAT).astype(F32)
                y = a * ws[0][:, i:i + 1] + b * ws[1][:, i:i + 1]
                mrg[k, i, dr] = y.astype(BF16).reshape(2, 8, LAT)
                merged(k, i, dr).start()

    def rs2(k, off):
        a2 = ORDERS[k][1]
        p = (co[a2] + off) % 4
        return rcopy(r1m.at[k, p, pl.ds(0, COUNT[k])], r2d.at[k, off - 1, pl.ds(0, COUNT[k])],
                     c_s.at[k, off - 1], c_r.at[k, off - 1], at(a2, p))

    def rs2_lse(k, off):
        a2 = ORDERS[k][1]
        p = (co[a2] + off) % 4
        return rcopy(lse1.at[k, pl.ds(p * 8, 8)], r2l.at[k, off - 1],
                     cl_s.at[k, off - 1], cl_r.at[k, off - 1], at(a2, p))

    for k in KS:
        base = co[ORDERS[k][2]] * 4
        for dr in DIRS:
            dir_lse(k, dr).wait_recv()
        ws, l1 = _merge_weights([lcol[k, pl.ds(base * 8, 32), :], r1dl[k, 0], r1dl[k, 1]])
        lse1[k] = l1
        for off in RING_OFFS:
            rs2_lse(k, off).start()
        for i in range(COUNT[k]):
            for dr in DIRS:
                plain(k, i, dr).wait_recv()
                merged(k, i, dr).wait_recv()
            y = obuf[k, i, pl.ds(base, 4)].reshape(32, LAT).astype(F32) * ws[0][:, i:i + 1]
            for dr in DIRS:
                y = y + r1d[k, i, dr].reshape(32, LAT).astype(F32) * ws[1 + dr][:, i:i + 1]
            y = y.astype(BF16).reshape(4, 8, LAT)
            for p in RING:
                r1m[k, p, i] = y[p]
        for off in (2, 1, 3):
            rs2(k, off).start()

    def rs3(k, off):
        a1 = ORDERS[k][0]
        j0 = co[a1] * 2 + core
        j = (j0 + off) % 8
        return rcopy(s3src.at[k, j], r3d.at[k, j0], e_s.at[k, off], e_r.at[k, off], line(a1, j))

    def rs3_lse(k, off):
        a1 = ORDERS[k][0]
        j0 = co[a1] * 2 + core
        j = (j0 + off) % 8
        return rcopy(s3l.at[k, j], r3l.at[k, j0], el_s.at[k, off], el_r.at[k, off], line(a1, j))

    def got3(k, off):
        j0 = co[ORDERS[k][0]] * 2 + core
        src = (j0 + 8 - off) % 8
        rcopy(s3src.at[k, 0], r3d.at[k, src], e_s.at[k, off], e_r.at[k, off], partner).wait_recv()
        rcopy(s3l.at[k, 0], r3l.at[k, src], el_s.at[k, off], el_r.at[k, off], partner).wait_recv()

    for k in KS:
        p2 = co[ORDERS[k][1]]
        n = COUNT[k]
        for off in RING_OFFS:
            rs2_lse(k, off).wait_recv()
        ws, l2 = _merge_weights([lse1[k, pl.ds(p2 * 8, 8), :]] + [r2l[k, x] for x in KS])
        lt = l2.T[0:8, :]
        for j in range(8):
            s3l[k, j] = jnp.broadcast_to(lt[:, j:j + 1], (8, LANES))
        for off in LINE_OFFS:
            rs3_lse(k, off).start()
        for off in RING_OFFS:
            rs2(k, off).wait_recv()
        ys = []
        for i in range(n):
            y = r1m[k, p2, i].astype(F32) * ws[0][:, i:i + 1]
            for x in KS:
                y = y + r2d[k, x, i].astype(F32) * ws[1 + x][:, i:i + 1]
            ys.append(y)
        y = jnp.concatenate(ys, axis=0).astype(BF16)
        pm = _perm(64, 8 * n, lambda r, c: (c == (r % 8) * 8 + r // 8) & (r % 8 < n))
        s3src[k] = jnp.dot(pm, y, preferred_element_type=F32).astype(BF16).reshape(8, 8, LAT)
        for off in LINE_OFFS:
            rs3(k, off).start()
        j0 = co[ORDERS[k][0]] * 2 + core
        r3d[k, j0] = s3src[k, j0]
        r3l[k, j0] = s3l[k, j0]

    outs = [[None] * 3 for _ in DIRS]
    for k in KS:
        for off in LINE_OFFS:
            got3(k, off)
        for h in DIRS:
            ws, _ = _merge_weights([r3l[k, 2 * p + h] for p in RING])
            y = None
            for p in RING:
                t = r3d[k, 2 * p + h].astype(F32) * jnp.concatenate([ws[p]] * 4, axis=1)
                y = t if y is None else y + t
            outs[h][k] = y
    rows = jnp.concatenate([outs[h][k] for h in DIRS for k in KS], axis=0).astype(BF16)
    fin = _perm(32, 48, lambda r, c: r == (c // 24) * 16 + 3 * (c % 8) + (c // 8) % 3)
    fin = jnp.where(_perm(32, 48, lambda r, c: 3 * (c % 8) + (c // 8) % 3 < 16) > 0, fin, jnp.zeros_like(fin))
    oout[...] = jnp.dot(fin, rows, preferred_element_type=F32).astype(BF16)
    store = pltpu.make_async_copy(oout, o_h, sem_o)
    store.start()

    for k in KS:
        for off in LINE_OFFS:
            rs3(k, off).wait_send()
            rs3_lse(k, off).wait_send()
        for off in RING_OFFS:
            rs2(k, off).wait_send()
            rs2_lse(k, off).wait_send()
        for dr in DIRS:
            opp_lse(k, dr).wait_send()
            dir_lse(k, dr).wait_send()

    def drain(k, i):
        for dr in DIRS:
            opp(k, i, dr).wait_send()
            plain(k, i, dr).wait_send()
            merged(k, i, dr).wait_send()

    each(drain)
    whole = q_all.at[0, 0]
    for off in KS:
        wait_bytes(whole, s2s.at[off])
    for off in RING:
        for dr in DIRS:
            wait_bytes(whole, s3s.at[dr, off])
        wait_bytes(whole, sfs.at[off])

    @pl.loop(0, 16)
    def _(s):
        push_cache(s).wait_send()

    store.wait()


def solution(mesh):
    def local(q, cache, lens):
        dma = pltpu.SemaphoreType.DMA
        V = pltpu.VMEM
        anyspace = pl.BlockSpec(memory_space=pl.ANY)
        scratch = [
            V((32, QW), BF16), V((2, 3, 8, QW), BF16), V((3, 8, 8, QW), BF16), V((3, NI, 16, 8, QW), BF16),
            V((16, 64, 8, QW), BF16), V((3, NI, 16, 8, LAT), BF16), V((3, LANES, LANES), F32), V((3, LANES, LANES), F32),
            V((3, NI, 2, 2, 8, LAT), BF16), V((3, 2, 16, LANES), F32), V((3, NI, 2, 2, 8, LAT), BF16),
            V((3, 2, 32, LANES), F32), V((3, NI, 2, 4, 8, LAT), BF16), V((3, 2, 32, LANES), F32),
            V((3, 4, NI, 8, LAT), BF16), V((3, 32, LANES), F32),
            V((3, 3, NI, 8, LAT), BF16), V((3, 3, 8, LANES), F32), V((3, 8, 8, LAT), BF16), V((3, 8, 8, LANES), F32),
            V((3, 8, 8, LAT), BF16), V((3, 8, 8, LANES), F32), V((32, LAT), BF16),
            dma, dma((16,)), dma((16,)), dma((16,)), dma((3, 8)), dma((3, 8)), dma((3,)), dma((3, NI, 3)),
            dma((2, 4)), dma((3, NI, 2, 4)), dma((4,)), dma((3, NI, 4)),
            dma((3, NI, 2)), dma((3, NI, 2)), dma((3, 2)), dma((3, 2)),
            dma((3, NI, 2, 2)), dma((3, NI, 2, 2)), dma((3, 2)), dma((3, 2)),
            dma((3, 3)), dma((3, 3)), dma((3, 3)), dma((3, 3)),
            dma((3, 8)), dma((3, 8)), dma((3, 8)), dma((3, 8)), dma,
        ]
        o = pl.pallas_call(
            _kernel,
            out_shape=jax.ShapeDtypeStruct((32, LAT), BF16),
            in_specs=[pl.BlockSpec(memory_space=pltpu.SMEM), anyspace, anyspace],
            out_specs=anyspace,
            scratch_shapes=scratch,
            compiler_params=pltpu.CompilerParams(collective_id=0, has_side_effects=True,
                                                 vmem_limit_bytes=58 * 2 ** 20),
        )(lens, q.reshape(32, QW), cache.reshape(32, 32, 8, QW))
        return o.reshape(32, 1, LAT)

    return jax.shard_map(local, mesh=mesh,
                         in_specs=(P('dp', 'dcp', None), P('dp', None, 'dcp', None, None), P('dp')),
                         out_specs=P('dp', 'dcp', None), check_vma=False)
```

time: 193 us -> 67.1 us (0.35)
  waiting for transfers between devices: 132 us -> 0 us
  Pallas kernels: 0 us -> 65.5 us
  matrix products: 16.9 us -> 0 us
  starting transfers between devices: 15.7 us -> 0 us
  between operations: 13.5 us -> 0.01 us
  other arithmetic: 7.92 us -> 0 us
  local copies, waits for them, and re-layouts: 5.12 us -> 1.38 us
    all_gather x1 -> x0, waiting for transfers between devices: 73.4 us -> none  [local(): qa = lax.all_gather(q, 'dcp', axis=1, tiled=True)]
    pallas_call x0 -> x1, Pallas kernels: none -> 65.5 us  [local(): pl.pallas_call(_kernel, out_shape=jax.ShapeDtypeStruct((32, LAT), BF16),...]
    all_to_all x2 -> x0, waiting for transfers between devices: 58.3 us -> none  [the longest x1 58.3 us: local(): od = lax.all_to_all(od.reshape(b, n, hl, lorav), 'dcp', 1, 1, tiled=True)]
    dot_general x2 -> x0, matrix products: 16.9 us -> none  [the longest x1 11 us: local(): jnp.einsum('bhk,btk->bht', qa, c, preferred_element_type=jnp.float32)]
    all_to_all x2 -> x0, starting transfers between devices: 15.7 us -> none  [the longest x1 10.2 us: local(): od = lax.all_to_all(od.reshape(b, n, hl, lorav), 'dcp', 1, 1, tiled=True)]
    reduce_sum x3 -> x0, other arithmetic: 6.24 us -> none  [the longest x1 3.36 us: local(): l = jnp.sum(p, axis=2)]
    reshape x1 -> x0, local copies, waits for them, and re-layouts: 4.3 us -> none  [local(): od = lax.all_to_all(od.reshape(b, n, hl, lorav), 'dcp', 1, 1, tiled=True)]
  transfers between devices with their start and end apart: 3 -> 0, of which waited for: 2 -> 0; matrix products, arithmetic and copies ran while one was open for 6% -> 0% of each run, Pallas kernels for 0% -> 0%
where the time goes in v1:
time: 67.1 us; the launch traced here: 66.9 us
  Pallas kernels  65.5 us (98%)
  local copies, waits for them, and re-layouts  1.38 us (2%)
    pallas_call x1, Pallas kernels, local(): pl.pallas_call(_kernel, out_shape=jax.ShapeDtypeStruct((32, LAT), BF16),...  65.5 us
    unnamed x1, local copies, waits for them, and re-layouts  1.38 us

profile of v1, /device:TPU:1, one launch (start us, length us, event | category | flops | bytes accessed | tf_op | source)
XLA Modules:
  0.0 66.9 jit_solution(7379253427240449084)
XLA Ops:
  0.0 65.5 %shard_map.37 = bf16[32,512]{1,0:T(8,128)(2,1)} custom-call(s32[32]{0:T(128)} %lens.1, bf16[32,576]{1,0:T(8,128)(2,1)} %bitcast.5, bf16[32,32,8,576]{3,2,1,0:T(8,128)(2,1)} %bitcast.3), custom_call_target="tpu_custom_call" | custom-call | tf_op jit(solution)/shard_map/pallas_call | solution.py:457
  65.5 1.4 %copy.5 = bf16[32,1,512]{2,0,1:T(8,128)(2,1)} copy(bf16[32,1,512]{2,0,1:T(8,128)(2,1)} %bitcast.4) | data formatting | bytes 65536

commit v2 on v0

v2 whole, which is shorter than its diff:
```python
import functools
import math

import jax
import jax.numpy as jnp
from jax import lax
from jax.experimental import pallas as pl
from jax.experimental.pallas import tpu as pltpu
from jax.sharding import PartitionSpec as P

ROPE = 64
QK_DIM = 192
SCALE2 = QK_DIM ** -0.5 * math.log2(math.e)
NEG = -3.0e38
MESH = pl.DeviceIdType.MESH
F32 = jnp.float32
BF16 = jnp.bfloat16

STRIDE = (2, 8, 32)
ORDERS = ((0, 1, 2), (1, 2, 0), (2, 0, 1))
COUNT = (6, 5, 5)
NI = 6
SPLIT, DIRECT, EARLY = 3, 2, 4


LAT, QW, LANES = 512, 576, 128
KS, DIRS, RING, RING_OFFS, LINE_OFFS = range(3), range(2), range(4), range(1, 4), range(1, 8)


def _perm(rows, cols, f):
    r = lax.broadcasted_iota(jnp.int32, (rows, cols), 0)
    c = lax.broadcasted_iota(jnp.int32, (rows, cols), 1)
    return f(r, c).astype(F32).astype(BF16)


def _merge_weights(lses):
    top = functools.reduce(jnp.maximum, lses)
    ws = [jnp.exp2(v - top) for v in lses]
    tot = functools.reduce(jnp.add, ws)
    inv = 1.0 / tot
    return [w * inv for w in ws], top + jnp.log2(tot)


def _kernel(lens, q_h, c_h, o_h,
            q_in, s1src, s1buf, q_all, cbuf, obuf, lrow, lcol, r1o, r1d, r1l, r1m, lse1,
            r2d, r2l, s3src, s3l, r3d, r3l, oout,
            sem_q, sem_o, c_s, c_r, s1_s, s1_r, s2_s, s2_r, s3_s, s3f_r, s3_r, sf_s,
            ro_s, ro_r, r1_s, r1_r, r1l_s, r1l_r, r2_s, r2_r, r2l_s, r2l_r, r3_s, r3_r, r3l_s, r3l_r):
    d = lax.axis_index('dcp')
    core = d % 2
    co = ((d // 2) % 4, (d // 8) % 4, d // 32)
    partner = {'dcp': d + 1 - 2 * core}

    def ring(axis, off):
        return {'dcp': d + ((co[axis] + off) % 4 - co[axis]) * STRIDE[axis]}

    def line(axis, j):
        return {'dcp': d + (j // 2 - co[axis]) * STRIDE[axis] + (j % 2 - core)}

    def send(src, dst, ss, rs, dev):
        pltpu.make_async_remote_copy(src_ref=src, dst_ref=dst, send_sem=ss, recv_sem=rs,
                                     device_id=dev, device_id_type=MESH).start()

    def wait(ref, sem):
        pltpu.make_async_copy(ref, ref, sem).wait()

    def ks_of(i):
        return KS if i < NI - 1 else range(1)

    load_q = pltpu.make_async_copy(q_h, q_in, sem_q)
    load_q.start()

    def cache_rows(i, half):
        n = len(ks_of(i))
        return c_h.at[pl.ds(16 * half + 3 * i, n)], cbuf.at[pl.ds(3 * i, n), pl.ds(32 * core, 32)]

    for i in range(NI):
        src, dst = cache_rows(i, core)
        pltpu.make_async_copy(src, dst, c_r.at[i]).start()

    bar = pltpu.get_barrier_semaphore()
    pl.semaphore_signal(bar, inc=1, device_id=partner, device_id_type=MESH)
    for a in KS:
        for off in RING_OFFS:
            for c2 in DIRS:
                pl.semaphore_signal(bar, inc=1, device_id=line(a, ((co[a] + off) % 4) * 2 + c2), device_id_type=MESH)
    lrow[...] = jnp.zeros_like(lrow)

    def sel(r, c):
        s = 3 * (r % 8) + (r // 8) % 3
        return (c == 16 * (r // 24) + s) & (s < 16)

    load_q.wait()
    qp = jnp.dot(_perm(48, 32, sel), q_in[...], preferred_element_type=F32).astype(BF16)
    s1src[...] = qp.reshape(2, 3, 8, QW)
    pl.semaphore_wait(bar, 19)

    def place(k):
        return co[ORDERS[k][0]] * 2 + core

    for k in KS:
        j0 = place(k)
        for off in LINE_OFFS:
            j = (j0 + off) % 8
            send(s1src.at[j % 2, k], s1buf.at[k, j0], s1_s, s1_r.at[k], line(ORDERS[k][0], j))
        s1buf[k, j0] = s1src[core, k]
    for i in range(NI):
        src, dst = cache_rows(i, 1 - core)
        send(src, dst, c_s, c_r.at[i], partner)

    def slot(k, i):
        return (k * NI + i) * 16

    def blk(k, i, off):
        _, a2, a3 = ORDERS[k]
        return q_all.at[slot(k, i) + co[a3] * 4 + (co[a2] - off) % 4]

    def copy3(k, i, off):
        b = blk(k, i, off)
        a3 = ORDERS[k][2]
        for o in (1, 3):
            fw = i >= DIRECT and off // 2 == o // 2
            send(b, b, s3_s, s3f_r.at[i] if fw else s3_r.at[i], ring(a3, o))
        if i < DIRECT:
            send(b, b, s3_s, s3_r.at[i], ring(a3, 2))

    def stage2(k, i):
        b = blk(k, i, 0)
        for off in (2, 1, 3):
            send(b, b, s2_s, s2_r.at[i], ring(ORDERS[k][1], off))
        copy3(k, i, 0)

    tr = _perm(64, 64, lambda r, c: (r // 8 == c % 8) & (r % 8 == c // 8))
    for k in KS:
        wait(s1buf.at[k, pl.ds(0, 7)], s1_r.at[k])
        rows = jnp.dot(tr, s1buf[k].reshape(64, QW), preferred_element_type=F32).astype(BF16).reshape(8, 8, QW)
        _, a2, a3 = ORDERS[k]
        for i in range(COUNT[k]):
            q_all[slot(k, i) + co[a3] * 4 + co[a2]] = rows[i]
        for i in range(EARLY):
            stage2(k, i)

    def stage3(i):
        n = len(ks_of(i))
        wait(q_all.at[pl.ds(0, 3 * n)], s2_r.at[i])
        for off in (1, 3, 2):
            for k in ks_of(i):
                copy3(k, i, off)

    def more2(i):
        for k in ks_of(i):
            stage2(k, i)

    def forward(i):
        n = len(ks_of(i))
        wait(q_all.at[pl.ds(0, 4 * n)], s3f_r.at[i])
        for off in RING:
            for k in ks_of(i):
                _, a2, a3 = ORDERS[k]
                o = 1 if off < 2 else 3
                b = q_all.at[slot(k, i) + ((co[a3] - o) % 4) * 4 + (co[a2] - off) % 4]
                send(b, b, sf_s, s3_r.at[i], ring(a3, o))

    def arrive(i):
        n = len(ks_of(i))
        wait(cbuf.at[pl.ds(0, n)], c_r.at[i])
        wait(q_all.at[pl.ds(0, (12 if i < DIRECT else 8) * n)], s3_r.at[i])

    for i in range(EARLY):
        stage3(i)
        if EARLY + i < NI:
            more2(EARLY + i)

    chip8 = (d // 2) * 16

    def attend(k, i):
        s = 3 * i + k
        n = lens[16 * core + s]
        cs = cbuf[s].reshape(LAT, QW)
        qs = q_all[pl.ds(slot(k, i), 16)].reshape(LANES, QW)
        st = lax.dot_general(cs, qs, (((1,), (1,)), ((), ())), preferred_element_type=F32) * SCALE2
        j = lax.broadcasted_iota(jnp.int32, (LAT, LANES), 0)
        ok = (j & 7) + ((j >> 3) & 31) * 1024 + (j >> 8) * 8 + chip8 < n
        st = jnp.where(ok, st, NEG)
        m = jnp.max(st, axis=0, keepdims=True)
        p = jnp.where(ok, jnp.exp2(st - m), 0.0)
        l = jnp.sum(p, axis=0, keepdims=True)
        has = l > 0.0
        ls = jnp.where(has, l, 1.0)
        pn = (p * (1.0 / ls)).astype(BF16)
        o = lax.dot_general(pn, cs[:, :LAT], (((0,), (0,)), ((), ())), preferred_element_type=F32)
        obuf[pl.ds(slot(k, i), 16)] = o.astype(BF16).reshape(16, 8, LAT)
        lrow[k, i:i + 1, :] = jnp.where(has, m + jnp.log2(ls), NEG)

    def wave(i):
        return 0 if i < SPLIT else 1

    def send1(k, i):
        a3 = ORDERS[k][2]
        w = wave(i)
        for o in RING_OFFS:
            g = slot(k, i) + ((co[a3] + o) % 4) * 4
            if o == 2 and w == 0:
                for h in DIRS:
                    send(obuf.at[pl.ds(g + 2 * h, 2)], r1o.at[k, i, h], r1_s, ro_r.at[i], ring(a3, 1 + 2 * h))
            else:
                send(obuf.at[pl.ds(g, 4)], r1d.at[k, i, o - 1], r1_s, r1_r.at[w, k], ring(a3, o))

    def relay(i):
        wait(obuf.at[pl.ds(0, 4 * len(KS))], ro_r.at[i])
        for k in KS:
            for h in DIRS:
                send(r1o.at[k, i, h], r1d.at[k, i, 1, pl.ds(2 * h, 2)], ro_s, r1_r.at[0, k], ring(ORDERS[k][2], 1 + 2 * h))

    def members(w, k):
        return range(SPLIT) if w == 0 else range(SPLIT, COUNT[k])

    def send1_lse(w):
        for k in KS:
            lcol[w, k] = lrow[k].T
            for o in RING_OFFS:
                p = (co[ORDERS[k][2]] + o) % 4
                send(lcol.at[w, k, pl.ds(p * 32, 32)], r1l.at[w, k, o - 1], r1l_s, r1l_r.at[w, k], ring(ORDERS[k][2], o))

    for i in range(NI):
        with jax.named_scope(f"arrive{i}"):
            arrive(i)
        with jax.named_scope(f"attend{i}"):
            for k in ks_of(i):
                attend(k, i)
            for k in ks_of(i):
                send1(k, i)
        with jax.named_scope(f"rest{i}"):
            if i == SPLIT - 1:
                send1_lse(0)
            if 0 < i <= SPLIT:
                relay(i - 1)
            if DIRECT <= i + 2 < NI:
                forward(i + 2)
            if EARLY + i < NI:
                stage3(EARLY + i)
            if 2 * EARLY + i < NI:
                more2(2 * EARLY + i)

    send1_lse(1)

    def merge1(w, k):
        a2, a3 = ORDERS[k][1:]
        its = members(w, k)
        wait(r1l.at[w, k], r1l_r.at[w, k])
        ws, l1 = _merge_weights([lcol[w, k, pl.ds(co[a3] * 32, 32), :]] + [r1l[w, k, x] for x in KS])
        lse1[w, k] = l1
        for o in RING_OFFS:
            p = (co[a2] + o) % 4
            send(lse1.at[w, k, pl.ds(p * 8, 8)], r2l.at[w, k, o - 1], r2l_s, r2l_r.at[w, k], ring(a2, o))
        wait(obuf.at[pl.ds(0, 12 * len(its))], r1_r.at[w, k])
        for i in its:
            y = obuf[pl.ds(slot(k, i) + co[a3] * 4, 4)].reshape(32, LAT).astype(F32) * ws[0][:, i:i + 1]
            for x in KS:
                y = y + r1d[k, i, x].reshape(32, LAT).astype(F32) * ws[1 + x][:, i:i + 1]
            y = y.astype(BF16).reshape(4, 8, LAT)
            for p in RING:
                r1m[k, p, i] = y[p]
        for o in (2, 1, 3):
            p = (co[a2] + o) % 4
            sl = pl.ds(its[0], len(its))
            send(r1m.at[k, p, sl], r2d.at[k, o - 1, sl], r2_s, r2_r.at[w, k], ring(a2, o))

    def merge2(w, k):
        a1, a2, _ = ORDERS[k]
        its = members(w, k)
        n = len(its)
        j0 = place(k)
        wait(r2l.at[w, k], r2l_r.at[w, k])
        ws, l2 = _merge_weights([lse1[w, k, pl.ds(co[a2] * 8, 8), :]] + [r2l[w, k, x] for x in KS])
        lt = l2.T[0:8, :]
        for j in range(8):
            s3l[w, k, j] = jnp.broadcast_to(lt[:, j:j + 1], (8, LANES))
        for off in LINE_OFFS:
            j = (j0 + off) % 8
            send(s3l.at[w, k, j], r3l.at[w, k, j0], r3l_s, r3l_r.at[w, k], line(a1, j))
        wait(obuf.at[pl.ds(0, 3 * n)], r2_r.at[w, k])
        ys = []
        for i in its:
            y = r1m[k, co[a2], i].astype(F32) * ws[0][:, i:i + 1]
            for x in KS:
                y = y + r2d[k, x, i].astype(F32) * ws[1 + x][:, i:i + 1]
            ys.append(y)
        y = jnp.concatenate(ys, axis=0).astype(BF16)
        lo = its[0]
        pm = _perm(64, 8 * n, lambda r, c: (c == (r % 8 - lo) * 8 + r // 8) & (r % 8 >= lo) & (r % 8 < lo + n))
        s3src[w, k] = jnp.dot(pm, y, preferred_element_type=F32).astype(BF16).reshape(8, 8, LAT)
        for off in LINE_OFFS:
            j = (j0 + off) % 8
            send(s3src.at[w, k, j], r3d.at[w, k, j0], r3_s, r3_r.at[w, k], line(a1, j))
        r3d[w, k, j0] = s3src[w, k, j0]
        r3l[w, k, j0] = s3l[w, k, j0]

    rows = {}

    def merge3(w, k):
        wait(r3l.at[w, k, pl.ds(0, 7)], r3l_r.at[w, k])
        wait(r3d.at[w, k, pl.ds(0, 7)], r3_r.at[w, k])
        for h in DIRS:
            ws, _ = _merge_weights([r3l[w, k, 2 * p + h] for p in RING])
            y = None
            for p in RING:
                t = r3d[w, k, 2 * p + h].astype(F32) * jnp.concatenate([ws[p]] * 4, axis=1)
                y = t if y is None else y + t
            rows[w, h, k] = y

    for k in KS:
        merge1(0, k)
    for k in KS:
        merge1(1, k)
    for k in KS:
        merge2(0, k)
    for k in KS:
        merge2(1, k)
    for k in KS:
        merge3(0, k)
    for k in KS:
        merge3(1, k)
    flat = jnp.concatenate([rows[w, h, k] for w in DIRS for h in DIRS for k in KS], axis=0).astype(BF16)

    def pick(r, c):
        w, h, k, i = c // 48, (c // 24) % 2, (c // 8) % 3, c % 8
        s = 3 * i + k
        return (r == 16 * h + s) & (s < 16) & ((i >= SPLIT) == (w == 1))

    oout[...] = jnp.dot(_perm(32, 96, pick), flat, preferred_element_type=F32).astype(BF16)
    store = pltpu.make_async_copy(oout, o_h, sem_o)
    store.start()

    wait(cbuf.at[pl.ds(0, 8)], c_s)
    wait(q_all.at[pl.ds(0, 21)], s1_s)
    wait(q_all.at[pl.ds(0, 48)], s2_s)
    wait(q_all.at[pl.ds(0, 128 + 4 * DIRECT * len(KS))], s3_s)
    wait(q_all.at[pl.ds(0, 4 * (16 - DIRECT * len(KS)))], sf_s)
    wait(obuf.at[pl.ds(0, 192)], r1_s)
    wait(obuf.at[pl.ds(0, 4 * len(KS) * SPLIT)], ro_s)
    wait(r1l, r1l_s)
    wait(obuf.at[pl.ds(0, 48)], r2_s)
    wait(r2l, r2l_s)
    for w in DIRS:
        for k in KS:
            wait(r3d.at[w, k, pl.ds(0, 7)], r3_s)
            wait(r3l.at[w, k, pl.ds(0, 7)], r3l_s)
    store.wait()


def solution(mesh):
    def local(q, cache, lens):
        dma = pltpu.SemaphoreType.DMA
        V = pltpu.VMEM
        anyspace = pl.BlockSpec(memory_space=pl.ANY)
        tile, qtile = (8, LAT), (8, QW)
        line = (2, 3, 8)
        scratch = [
            V((32, QW), BF16), V((2, 3) + qtile, BF16), V((3, 8) + qtile, BF16), V((288,) + qtile, BF16),
            V((16, 64) + qtile, BF16), V((288,) + tile, BF16), V((3, LANES, LANES), F32), V((2, 3, LANES, LANES), F32),
            V((3, SPLIT, 2, 2) + tile, BF16), V((3, NI, 3, 4) + tile, BF16), V((2, 3, 3, 32, LANES), F32),
            V((3, 4, NI) + tile, BF16), V((2, 3, 32, LANES), F32),
            V((3, 3, NI) + tile, BF16), V((2, 3, 3, 8, LANES), F32),
            V(line + tile, BF16), V(line + (8, LANES), F32), V(line + tile, BF16), V(line + (8, LANES), F32),
            V((32, LAT), BF16),
            dma, dma, dma, dma((NI,)), dma, dma((3,)), dma, dma((NI,)), dma, dma((NI,)), dma((NI,)), dma,
            dma, dma((SPLIT,)), dma, dma((2, 3)), dma, dma((2, 3)), dma, dma((2, 3)), dma, dma((2, 3)),
            dma, dma((2, 3)), dma, dma((2, 3)),
        ]
        o = pl.pallas_call(
            _kernel,
            out_shape=jax.ShapeDtypeStruct((32, LAT), BF16),
            in_specs=[pl.BlockSpec(memory_space=pltpu.SMEM), anyspace, anyspace],
            out_specs=anyspace,
            scratch_shapes=scratch,
            compiler_params=pltpu.CompilerParams(collective_id=0, has_side_effects=True,
                                                 vmem_limit_bytes=58 * 2 ** 20),
        )(lens, q.reshape(32, QW), cache.reshape(32, 32, 8, QW))
        return o.reshape(32, 1, LAT)

    return jax.shard_map(local, mesh=mesh,
                         in_specs=(P('dp', 'dcp', None), P('dp', None, 'dcp', None, None), P('dp')),
                         out_specs=P('dp', 'dcp', None), check_vma=False)
```

time: 193 us -> 56.6 us (0.29)
  waiting for transfers between devices: 132 us -> 0 us
  Pallas kernels: 0 us -> 55 us
  matrix products: 16.9 us -> 0 us
  starting transfers between devices: 15.7 us -> 0 us
  between operations: 13.5 us -> 0.01 us
  other arithmetic: 7.92 us -> 0 us
  local copies, waits for them, and re-layouts: 5.12 us -> 1.38 us
    all_gather x1 -> x0, waiting for transfers between devices: 73.4 us -> none  [local(): qa = lax.all_gather(q, 'dcp', axis=1, tiled=True)]
    all_to_all x2 -> x0, waiting for transfers between devices: 58.3 us -> none  [the longest x1 58.3 us: local(): od = lax.all_to_all(od.reshape(b, n, hl, lorav), 'dcp', 1, 1, tiled=True)]
    pallas_call x0 -> x1, Pallas kernels: none -> 55 us  [local(): pl.pallas_call(_kernel, out_shape=jax.ShapeDtypeStruct((32, LAT), BF16),...]
    dot_general x2 -> x0, matrix products: 16.9 us -> none  [the longest x1 11 us: local(): jnp.einsum('bhk,btk->bht', qa, c, preferred_element_type=jnp.float32)]
    all_to_all x2 -> x0, starting transfers between devices: 15.7 us -> none  [the longest x1 10.2 us: local(): od = lax.all_to_all(od.reshape(b, n, hl, lorav), 'dcp', 1, 1, tiled=True)]
    reduce_sum x3 -> x0, other arithmetic: 6.24 us -> none  [the longest x1 3.36 us: local(): l = jnp.sum(p, axis=2)]
    reshape x1 -> x0, local copies, waits for them, and re-layouts: 4.3 us -> none  [local(): od = lax.all_to_all(od.reshape(b, n, hl, lorav), 'dcp', 1, 1, tiled=True)]
  transfers between devices with their start and end apart: 3 -> 0, of which waited for: 2 -> 0; matrix products, arithmetic and copies ran while one was open for 6% -> 0% of each run, Pallas kernels for 0% -> 0%
where the time goes in v2:
time: 56.6 us; the launch traced here: 56.4 us
  Pallas kernels  55 us (97%)
  local copies, waits for them, and re-layouts  1.38 us (2%)
    pallas_call x1, Pallas kernels, local(): pl.pallas_call(_kernel, out_shape=jax.ShapeDtypeStruct((32, LAT), BF16),...  55 us
    unnamed x1, local copies, waits for them, and re-layouts  1.38 us

profile of v2, /device:TPU:1, one launch (start us, length us, event | category | flops | bytes accessed | tf_op | source)
XLA Modules:
  0.0 56.4 jit_solution(8286613250391515628)
XLA Ops:
  0.0 55.0 %shard_map.37 = bf16[32,512]{1,0:T(8,128)(2,1)} custom-call(s32[32]{0:T(128)} %lens.1, bf16[32,576]{1,0:T(8,128)(2,1)} %bitcast.5, bf16[32,32,8,576]{3,2,1,0:T(8,128)(2,1)} %bitcast.3), custom_call_target="tpu_custom_call" | custom-call | tf_op jit(solution)/shard_map/pallas_call | solution.py:371
  55.0 1.4 %copy.5 = bf16[32,1,512]{2,0,1:T(8,128)(2,1)} copy(bf16[32,1,512]{2,0,1:T(8,128)(2,1)} %bitcast.4) | data formatting | bytes 65536

commit v3 on v2

v3 whole, which is shorter than its diff:
```python
import functools
import math

import jax
import jax.numpy as jnp
from jax import lax
from jax.experimental import pallas as pl
from jax.experimental.pallas import tpu as pltpu
from jax.sharding import PartitionSpec as P

ROPE = 64
QK_DIM = 192
SCALE2 = QK_DIM ** -0.5 * math.log2(math.e)
NEG = -3.0e38
MESH = pl.DeviceIdType.MESH
F32 = jnp.float32
BF16 = jnp.bfloat16

STRIDE = (2, 8, 32)
ORDERS = ((0, 1, 2), (1, 2, 0), (2, 0, 1))
COUNT = (6, 5, 5)
NI = 6
SPLIT, DIRECT, EARLY = 3, 2, 4


LAT, QW, LANES = 512, 576, 128
KS, DIRS, RING, RING_OFFS, LINE_OFFS = range(3), range(2), range(4), range(1, 4), range(1, 8)


def _perm(rows, cols, f):
    r = lax.broadcasted_iota(jnp.int32, (rows, cols), 0)
    c = lax.broadcasted_iota(jnp.int32, (rows, cols), 1)
    return f(r, c).astype(F32).astype(BF16)


def _merge_weights(lses):
    top = functools.reduce(jnp.maximum, lses)
    ws = [jnp.exp2(v - top) for v in lses]
    tot = functools.reduce(jnp.add, ws)
    inv = 1.0 / tot
    return [w * inv for w in ws], top + jnp.log2(tot)


def _kernel(lens_h, q_h, c_h, o_h,
            lens, q_in, s1src, s1buf, q_even, q_odd, cbuf, obuf, lrow, wcol, r1d, r1l, r1m, lse1,
            r2d, r2l, s3src, s3l, r3d, r3l, oout,
            sem_l, sem_q, sem_o, c_s, c_r, s1_s, s1_r, s2_s, s2_r, s3_s, s3f_r, s3_r, sf_s,
            r1_s, r1_r, r1l_s, r1l_r, r2_s, r2_r, r2l_s, r2l_r, r3_s, r3_r, r3l_s, r3l_r):
    d = lax.axis_index('dcp')
    core = d % 2
    co = ((d // 2) % 4, (d // 8) % 4, d // 32)
    partner = {'dcp': d + 1 - 2 * core}

    def ring(axis, off):
        return {'dcp': d + ((co[axis] + off) % 4 - co[axis]) * STRIDE[axis]}

    def line(axis, j):
        return {'dcp': d + (j // 2 - co[axis]) * STRIDE[axis] + (j % 2 - core)}

    def send(src, dst, ss, rs, dev):
        pltpu.make_async_remote_copy(src_ref=src, dst_ref=dst, send_sem=ss, recv_sem=rs,
                                     device_id=dev, device_id_type=MESH).start()

    def wait(ref, sem):
        pltpu.make_async_copy(ref, ref, sem).wait()

    def ks_of(i):
        return KS if i < NI - 1 else range(1)

    load_q = pltpu.make_async_copy(q_h, q_in, sem_q)
    load_q.start()
    load_l = pltpu.make_async_copy(lens_h, lens, sem_l)
    load_l.start()

    def cache_rows(i, half):
        n = len(ks_of(i))
        return c_h.at[pl.ds(16 * half + 3 * i, n)], cbuf.at[pl.ds(3 * i, n), pl.ds(32 * core, 32)]

    for i in range(NI):
        src, dst = cache_rows(i, core)
        pltpu.make_async_copy(src, dst, c_r.at[i]).start()

    bar = pltpu.get_barrier_semaphore()
    pl.semaphore_signal(bar, inc=1, device_id=partner, device_id_type=MESH)
    for a in KS:
        for off in RING_OFFS:
            for c2 in DIRS:
                pl.semaphore_signal(bar, inc=1, device_id=line(a, ((co[a] + off) % 4) * 2 + c2), device_id_type=MESH)
    lrow[...] = jnp.zeros_like(lrow)
    load_l.wait()

    def sel(r, c):
        s = 3 * (r % 8) + (r // 8) % 3
        return (c == 16 * (r // 24) + s) & (s < 16)

    load_q.wait()
    qp = jnp.dot(_perm(48, 32, sel), q_in[...], preferred_element_type=F32).astype(BF16)
    s1src[...] = qp.reshape(2, 3, 8, QW)
    pl.semaphore_wait(bar, 19)

    def place(k):
        return co[ORDERS[k][0]] * 2 + core

    for k in KS:
        j0 = place(k)
        for off in LINE_OFFS:
            j = (j0 + off) % 8
            send(s1src.at[j % 2, k], s1buf.at[k, j0], s1_s.at[k], s1_r.at[k], line(ORDERS[k][0], j))
        s1buf[k, j0] = s1src[core, k]
    for i in range(NI):
        src, dst = cache_rows(i, 1 - core)
        send(src, dst, c_s, c_r.at[i], partner)

    def q_of(i):
        return q_odd if i % 2 else q_even

    def q_slot(k, i):
        return (k * 3 + i // 2) * 16

    def slot(k, i):
        return (k * NI + i) * 16

    def blk(k, i, off):
        _, a2, a3 = ORDERS[k]
        return q_of(i).at[q_slot(k, i) + co[a3] * 4 + (co[a2] - off) % 4]

    def copy3(k, i, off):
        b = blk(k, i, off)
        a3 = ORDERS[k][2]
        for o in (1, 3):
            fw = i >= DIRECT and off // 2 == o // 2
            send(b, b, s3_s.at[i % 2], s3f_r.at[i] if fw else s3_r.at[i], ring(a3, o))
        if i < DIRECT:
            send(b, b, s3_s.at[i % 2], s3_r.at[i], ring(a3, 2))

    def stage2(k, i):
        b = blk(k, i, 0)
        for off in (2, 1, 3):
            send(b, b, s2_s.at[i % 2], s2_r.at[i], ring(ORDERS[k][1], off))
        copy3(k, i, 0)

    tr = _perm(64, 64, lambda r, c: (r // 8 == c % 8) & (r % 8 == c // 8))
    for k in KS:
        wait(s1buf.at[k, pl.ds(0, 7)], s1_r.at[k])
        rows = jnp.dot(tr, s1buf[k].reshape(64, QW), preferred_element_type=F32)
        _, a2, a3 = ORDERS[k]
        for i in range(COUNT[k]):
            y = rows[8 * i:8 * i + 8, :LAT if i % 2 else QW]
            if i % 2 == 0:
                y = jnp.concatenate([y, rows[8 * i + 8:8 * i + 16, LAT:]], axis=1)
            q_of(i)[q_slot(k, i) + co[a3] * 4 + co[a2]] = y.astype(BF16)
        for i in range(EARLY):
            stage2(k, i)

    def stage3(i):
        n = len(ks_of(i))
        wait(q_of(i).at[pl.ds(0, 3 * n)], s2_r.at[i])
        for off in (1, 3, 2):
            for k in ks_of(i):
                copy3(k, i, off)

    def more2(i):
        for k in ks_of(i):
            stage2(k, i)

    def forward(i):
        n = len(ks_of(i))
        wait(q_of(i).at[pl.ds(0, 4 * n)], s3f_r.at[i])
        for off in RING:
            for k in ks_of(i):
                _, a2, a3 = ORDERS[k]
                o = 1 if off < 2 else 3
                b = q_of(i).at[q_slot(k, i) + ((co[a3] - o) % 4) * 4 + (co[a2] - off) % 4]
                send(b, b, sf_s.at[i % 2], s3_r.at[i], ring(a3, o))

    def arrive(i):
        n = len(ks_of(i))
        wait(cbuf.at[pl.ds(0, n)], c_r.at[i])
        wait(q_of(i).at[pl.ds(0, (12 if i < DIRECT else 8) * n)], s3_r.at[i])

    for i in range(EARLY):
        stage3(i)
        if EARLY + i < NI:
            more2(EARLY + i)

    chip8 = (d // 2) * 16

    j = lax.broadcasted_iota(jnp.int32, (LAT, LANES), 0)
    pos = (j & 7) + ((j >> 3) & 31) * 1024 + (j >> 8) * 8

    def cache_of(k, i):
        return cbuf[3 * i + k].reshape(LAT, QW)

    def scores(k, i):
        cs = cache_of(k, i)
        n = pl.ds(q_slot(k, i), 16)
        lat = q_of(i)[n, :, :LAT].reshape(LANES, LAT)
        rope = q_even[n, :, LAT:].reshape(LANES, LANES)
        rope = rope[:, ROPE:] if i % 2 else rope[:, :ROPE]
        dims = (((1,), (1,)), ((), ()))
        st = lax.dot_general(cs[:, :LAT], lat, dims, preferred_element_type=F32)
        return (st + lax.dot_general(cs[:, LAT:], rope, dims, preferred_element_type=F32)) * SCALE2

    def softmax(st, k, i):
        ok = pos < lens[16 * core + 3 * i + k] - chip8
        st = jnp.where(ok, st, NEG)
        m = jnp.max(st, axis=0, keepdims=True)
        p = jnp.where(ok, jnp.exp2(st - m), 0.0)
        l = jnp.sum(p, axis=0, keepdims=True)
        has = l > 0.0
        ls = jnp.where(has, l, 1.0)
        w = wave(i)
        lrow[w, k, i - w * SPLIT:i - w * SPLIT + 1, :] = jnp.where(has, m + jnp.log2(ls), NEG)
        return (p * (1.0 / ls)).astype(BF16)

    def attend(i):
        ks = ks_of(i)
        sts = [scores(k, i) for k in ks]
        ps = [softmax(st, k, i) for st, k in zip(sts, ks)]
        outs = [lax.dot_general(p, cache_of(k, i)[:, :LAT], (((0,), (0,)), ((), ())), preferred_element_type=F32)
                for p, k in zip(ps, ks)]
        for o, k in zip(outs, ks):
            obuf[pl.ds(slot(k, i), 16)] = o.astype(BF16).reshape(16, 8, LAT)

    def wave(i):
        return 0 if i < SPLIT else 1

    def send1(k, i):
        a3 = ORDERS[k][2]
        for o in (2, 1, 3):
            b = obuf.at[pl.ds(slot(k, i) + ((co[a3] + o) % 4) * 4, 4)]
            send(b, r1d.at[k, i, o - 1], r1_s, r1_r.at[wave(i), k], ring(a3, o))

    def members(w, k):
        return range(SPLIT) if w == 0 else range(SPLIT, COUNT[k])

    def send1_lse(w):
        for k in KS:
            for o in RING_OFFS:
                send(lrow.at[w, k], r1l.at[w, k, o - 1], r1l_s, r1l_r.at[w, k], ring(ORDERS[k][2], o))

    for i in range(NI):
        with jax.named_scope(f"arrive{i}"):
            arrive(i)
        with jax.named_scope(f"attend{i}"):
            attend(i)
            for k in ks_of(i):
                send1(k, i)
        with jax.named_scope(f"rest{i}"):
            if i == SPLIT - 1:
                send1_lse(0)
            if DIRECT <= i + 2 < NI:
                forward(i + 2)
            if EARLY + i < NI:
                stage3(EARLY + i)
            if 2 * EARLY + i < NI:
                more2(2 * EARLY + i)

    send1_lse(1)

    def columns(ws, row, n):
        wcol[:, :32] = jnp.concatenate(ws, axis=0).T
        t = wcol[pl.ds(row, n), :32]
        return lambda x, i: t[:, 8 * x + i:8 * x + i + 1]

    def merge1(w, k):
        a2, a3 = ORDERS[k][1:]
        its = members(w, k)
        wait(r1l.at[w, k], r1l_r.at[w, k])
        ws, lse1[w, k] = _merge_weights([lrow[w, k]] + [r1l[w, k, x] for x in KS])
        for o in RING_OFFS:
            send(lse1.at[w, k], r2l.at[w, k, o - 1], r2l_s, r2l_r.at[w, k], ring(a2, o))
        cols = columns(ws, co[a3] * 32, 32)
        wait(obuf.at[pl.ds(0, 12 * len(its))], r1_r.at[w, k])
        for i in its:
            y = obuf[pl.ds(slot(k, i) + co[a3] * 4, 4)].reshape(32, LAT).astype(F32) * cols(0, i - its[0])
            for x in KS:
                y = y + r1d[k, i, x].reshape(32, LAT).astype(F32) * cols(1 + x, i - its[0])
            y = y.astype(BF16).reshape(4, 8, LAT)
            for p in RING:
                r1m[k, p, i] = y[p]
        for o in (2, 1, 3):
            p = (co[a2] + o) % 4
            sl = pl.ds(its[0], len(its))
            send(r1m.at[k, p, sl], r2d.at[k, o - 1, sl], r2_s, r2_r.at[w, k], ring(a2, o))

    def merge2(w, k):
        a1, a2, a3 = ORDERS[k]
        its = members(w, k)
        n = len(its)
        j0 = place(k)
        wait(r2l.at[w, k], r2l_r.at[w, k])
        ws, l2 = _merge_weights([lse1[w, k]] + [r2l[w, k, x] for x in KS])
        g = co[a3] * 4 + co[a2]
        lt = pltpu.roll(l2, ((16 - g) % 16) * 8, 1)
        cols = columns(ws, g * 8, 8)
        for j in range(8):
            s3l[w, k, j] = jnp.broadcast_to(lt[:, j:j + 1], (8, LANES))
        for off in LINE_OFFS:
            j = (j0 + off) % 8
            send(s3l.at[w, k, j], r3l.at[w, k, j0], r3l_s, r3l_r.at[w, k], line(a1, j))
        wait(obuf.at[pl.ds(0, 3 * n)], r2_r.at[w, k])
        ys = []
        for i in its:
            y = r1m[k, co[a2], i].astype(F32) * cols(0, i - its[0])
            for x in KS:
                y = y + r2d[k, x, i].astype(F32) * cols(1 + x, i - its[0])
            ys.append(y)
        y = jnp.concatenate(ys, axis=0).astype(BF16)
        pm = _perm(64, 8 * n, lambda r, c: (c == (r % 8) * 8 + r // 8) & (r % 8 < n))
        s3src[w, k] = jnp.dot(pm, y, preferred_element_type=F32).astype(BF16).reshape(8, 8, LAT)
        for off in LINE_OFFS:
            j = (j0 + off) % 8
            send(s3src.at[w, k, j], r3d.at[w, k, j0], r3_s, r3_r.at[w, k], line(a1, j))
        r3d[w, k, j0] = s3src[w, k, j0]
        r3l[w, k, j0] = s3l[w, k, j0]

    rows = {}

    def merge3(w, k):
        wait(r3l.at[w, k, pl.ds(0, 7)], r3l_r.at[w, k])
        wait(r3d.at[w, k, pl.ds(0, 7)], r3_r.at[w, k])
        for h in DIRS:
            ws, _ = _merge_weights([r3l[w, k, 2 * p + h] for p in RING])
            y = None
            for p in RING:
                t = r3d[w, k, 2 * p + h].astype(F32) * jnp.concatenate([ws[p]] * 4, axis=1)
                y = t if y is None else y + t
            rows[w, h, k] = y

    for k in KS:
        merge1(0, k)
    for k in KS:
        merge1(1, k)
    for k in KS:
        merge2(0, k)
    for k in KS:
        merge2(1, k)
    for k in KS:
        merge3(0, k)
    for k in KS:
        merge3(1, k)
    flat = jnp.concatenate([rows[w, h, k] for w in DIRS for h in DIRS for k in KS], axis=0).astype(BF16)

    def pick(r, c):
        w, h, k, i = c // 48, (c // 24) % 2, (c // 8) % 3, c % 8
        s = 3 * (i + w * SPLIT) + k
        return (r == 16 * h + s) & (s < 16) & (i < SPLIT)

    oout[...] = jnp.dot(_perm(32, 96, pick), flat, preferred_element_type=F32).astype(BF16)
    store = pltpu.make_async_copy(oout, o_h, sem_o)
    store.start()

    wait(cbuf.at[pl.ds(0, 8)], c_s)
    for k in KS:
        wait(s1buf.at[k, pl.ds(0, 7)], s1_s.at[k])
    for par in DIRS:
        its = [i for i in range(NI) for _ in ks_of(i) if i % 2 == par]
        wait(q_of(par).at[pl.ds(0, 3 * len(its))], s2_s.at[par])
        wait(q_of(par).at[pl.ds(0, sum(12 if i < DIRECT else 8 for i in its))], s3_s.at[par])
        wait(q_of(par).at[pl.ds(0, sum(0 if i < DIRECT else 4 for i in its))], sf_s.at[par])
    wait(obuf.at[pl.ds(0, 192)], r1_s)
    wait(r1l, r1l_s)
    wait(obuf.at[pl.ds(0, 48)], r2_s)
    wait(r2l, r2l_s)
    for w in DIRS:
        for k in KS:
            wait(r3d.at[w, k, pl.ds(0, 7)], r3_s)
            wait(r3l.at[w, k, pl.ds(0, 7)], r3l_s)
    store.wait()


def solution(mesh):
    def local(q, cache, lens):
        dma = pltpu.SemaphoreType.DMA
        V = pltpu.VMEM
        anyspace = pl.BlockSpec(memory_space=pl.ANY)
        tile, qtile, row = (8, LAT), (8, QW), (8, LANES)
        line = (2, 3, 8)
        scratch = [
            pltpu.SMEM((32,), jnp.int32), V((32, QW), BF16), V((2, 3) + qtile, BF16), V((3, 8) + qtile, BF16),
            V((144, 8, LAT + LANES), BF16), V((144,) + tile, BF16),
            V((16, 64) + qtile, BF16), V((288,) + tile, BF16), V((2, 3) + row, F32), V((LANES, LANES), F32),
            V((3, NI, 3, 4) + tile, BF16), V((2, 3, 3) + row, F32), V((3, 4, NI) + tile, BF16), V((2, 3) + row, F32),
            V((3, 3, NI) + tile, BF16), V((2, 3, 3) + row, F32),
            V(line + tile, BF16), V(line + row, F32), V(line + tile, BF16), V(line + row, F32),
            V((32, LAT), BF16),
            dma, dma, dma, dma, dma((NI,)), dma((3,)), dma((3,)), dma((2,)), dma((NI,)),
            dma((2,)), dma((NI,)), dma((NI,)), dma((2,)),
            dma, dma((2, 3)), dma, dma((2, 3)), dma, dma((2, 3)), dma, dma((2, 3)),
            dma, dma((2, 3)), dma, dma((2, 3)),
        ]
        o = pl.pallas_call(
            _kernel,
            out_shape=jax.ShapeDtypeStruct((32, LAT), BF16),
            in_specs=[anyspace] * 3,
            out_specs=anyspace,
            scratch_shapes=scratch,
            compiler_params=pltpu.CompilerParams(collective_id=0, has_side_effects=True,
                                                 vmem_limit_bytes=58 * 2 ** 20),
        )(lens, q.reshape(32, QW), cache.reshape(32, 32, 8, QW))
        return o.reshape(32, 1, LAT)

    return jax.shard_map(local, mesh=mesh,
                         in_specs=(P('dp', 'dcp', None), P('dp', None, 'dcp', None, None), P('dp')),
                         out_specs=P('dp', 'dcp', None), check_vma=False)
```

time: 56.6 us -> 52.5 us (0.928)
  Pallas kernels: 55 us -> 51 us
    pallas_call x1, Pallas kernels: 55 us -> 51 us  [local(): pl.pallas_call(_kernel, out_shape=jax.ShapeDtypeStruct((32, LAT), BF16),...]
where the time goes in v3:
time: 52.5 us; the launch traced here: 52.3 us
  Pallas kernels  51 us (97%)
  local copies, waits for them, and re-layouts  1.38 us (3%)
    pallas_call x1, Pallas kernels, local(): pl.pallas_call(_kernel, out_shape=jax.ShapeDtypeStruct((32, LAT), BF16),...  51 us
    unnamed x1, local copies, waits for them, and re-layouts  1.38 us

profile of v3, /device:TPU:1, one launch (start us, length us, event | category | flops | bytes accessed | tf_op | source)
XLA Modules:
  0.0 52.3 jit_solution(7843711406251208377)
XLA Ops:
  0.0 51.0 %shard_map.37 = bf16[32,512]{1,0:T(8,128)(2,1)} custom-call(s32[32]{0:T(128)} %lens_h.1, bf16[32,576]{1,0:T(8,128)(2,1)} %bitcast.5, bf16[32,32,8,576]{3,2,1,0:T(8,128)(2,1)} %bitcast.3), custom_call_target="tpu_custom_call" | custom-call | tf_op jit(solution)/shard_map/pallas_call | solution.py:393
  51.0 1.4 %copy.5 = bf16[32,1,512]{2,0,1:T(8,128)(2,1)} copy(bf16[32,1,512]{2,0,1:T(8,128)(2,1)} %bitcast.4) | data formatting | bytes 65536

commit v4 on v3

--- a/solution.py
+++ b/solution.py
@@ -20,7 +20,7 @@
 ORDERS = ((0, 1, 2), (1, 2, 0), (2, 0, 1))
 COUNT = (6, 5, 5)
 NI = 6
-SPLIT, DIRECT, EARLY = 3, 2, 4
+SPLIT, RELAYED = 3, 3
 
 
 LAT, QW, LANES = 512, 576, 128
@@ -127,11 +127,9 @@
     def copy3(k, i, off):
         b = blk(k, i, off)
         a3 = ORDERS[k][2]
-        for o in (1, 3):
-            fw = i >= DIRECT and off // 2 == o // 2
-            send(b, b, s3_s.at[i % 2], s3f_r.at[i] if fw else s3_r.at[i], ring(a3, o))
-        if i < DIRECT:
-            send(b, b, s3_s.at[i % 2], s3_r.at[i], ring(a3, 2))
+        for o in (2, 1, 3) if i < RELAYED else (1, 3):
+            onward = i >= RELAYED and off // 2 == o // 2
+            send(b, b, s3_s.at[i % 2], s3f_r.at[i] if onward else s3_r.at[i], ring(a3, o))
 
     def stage2(k, i):
         b = blk(k, i, 0)
@@ -149,7 +147,7 @@
             if i % 2 == 0:
                 y = jnp.concatenate([y, rows[8 * i + 8:8 * i + 16, LAT:]], axis=1)
             q_of(i)[q_slot(k, i) + co[a3] * 4 + co[a2]] = y.astype(BF16)
-        for i in range(EARLY):
+        for i in range(COUNT[k]):
             stage2(k, i)
 
     def stage3(i):
@@ -159,13 +157,8 @@
             for k in ks_of(i):
                 copy3(k, i, off)
 
-    def more2(i):
-        for k in ks_of(i):
-            stage2(k, i)
-
     def forward(i):
-        n = len(ks_of(i))
-        wait(q_of(i).at[pl.ds(0, 4 * n)], s3f_r.at[i])
+        wait(q_of(i).at[pl.ds(0, 4 * len(ks_of(i)))], s3f_r.at[i])
         for off in RING:
             for k in ks_of(i):
                 _, a2, a3 = ORDERS[k]
@@ -176,12 +169,10 @@
     def arrive(i):
         n = len(ks_of(i))
         wait(cbuf.at[pl.ds(0, n)], c_r.at[i])
-        wait(q_of(i).at[pl.ds(0, (12 if i < DIRECT else 8) * n)], s3_r.at[i])
-
-    for i in range(EARLY):
+        wait(q_of(i).at[pl.ds(0, (12 if i < RELAYED else 8) * n)], s3_r.at[i])
+
+    for i in range(NI):
         stage3(i)
-        if EARLY + i < NI:
-            more2(EARLY + i)
 
     chip8 = (d // 2) * 16
 
@@ -249,12 +240,9 @@
         with jax.named_scope(f"rest{i}"):
             if i == SPLIT - 1:
                 send1_lse(0)
-            if DIRECT <= i + 2 < NI:
-                forward(i + 2)
-            if EARLY + i < NI:
-                stage3(EARLY + i)
-            if 2 * EARLY + i < NI:
-                more2(2 * EARLY + i)
+            if i == 1:
+                for x in range(RELAYED, NI):
+                    forward(x)
 
     send1_lse(1)
 
@@ -334,10 +322,22 @@
         merge1(1, k)
     for k in KS:
         merge2(0, k)
+    wait(cbuf.at[pl.ds(0, 8)], c_s)
+    for k in KS:
+        wait(s1buf.at[k, pl.ds(0, 7)], s1_s.at[k])
+    for par in DIRS:
+        its = [i for i in range(NI) for _ in ks_of(i) if i % 2 == par]
+        wait(q_of(par).at[pl.ds(0, 3 * len(its))], s2_s.at[par])
+        wait(q_of(par).at[pl.ds(0, sum(12 if i < RELAYED else 8 for i in its))], s3_s.at[par])
+        wait(q_of(par).at[pl.ds(0, sum(0 if i < RELAYED else 4 for i in its))], sf_s.at[par])
     for k in KS:
         merge2(1, k)
     for k in KS:
         merge3(0, k)
+    wait(obuf.at[pl.ds(0, 192)], r1_s)
+    wait(r1l, r1l_s)
+    wait(obuf.at[pl.ds(0, 48)], r2_s)
+    wait(r2l, r2l_s)
     for k in KS:
         merge3(1, k)
     flat = jnp.concatenate([rows[w, h, k] for w in DIRS for h in DIRS for k in KS], axis=0).astype(BF16)
@@ -351,18 +351,6 @@
     store = pltpu.make_async_copy(oout, o_h, sem_o)
     store.start()
 
-    wait(cbuf.at[pl.ds(0, 8)], c_s)
-    for k in KS:
-        wait(s1buf.at[k, pl.ds(0, 7)], s1_s.at[k])
-    for par in DIRS:
-        its = [i for i in range(NI) for _ in ks_of(i) if i % 2 == par]
-        wait(q_of(par).at[pl.ds(0, 3 * len(its))], s2_s.at[par])
-        wait(q_of(par).at[pl.ds(0, sum(12 if i < DIRECT else 8 for i in its))], s3_s.at[par])
-        wait(q_of(par).at[pl.ds(0, sum(0 if i < DIRECT else 4 for i in its))], sf_s.at[par])
-    wait(obuf.at[pl.ds(0, 192)], r1_s)
-    wait(r1l, r1l_s)
-    wait(obuf.at[pl.ds(0, 48)], r2_s)
-    wait(r2l, r2l_s)
     for w in DIRS:
         for k in KS:
             wait(r3d.at[w, k, pl.ds(0, 7)], r3_s)

time: 52.5 us -> 47.7 us (0.909)
  Pallas kernels: 51 us -> 46.2 us
    pallas_call x1, Pallas kernels: 51 us -> 46.2 us  [local(): pl.pallas_call(_kernel, out_shape=jax.ShapeDtypeStruct((32, LAT), BF16),...]
where the time goes in v4:
time: 47.7 us; the launch traced here: 47.6 us
  Pallas kernels  46.2 us (97%)
  local copies, waits for them, and re-layouts  1.38 us (3%)
    pallas_call x1, Pallas kernels, local(): pl.pallas_call(_kernel, out_shape=jax.ShapeDtypeStruct((32, LAT), BF16),...  46.2 us
    unnamed x1, local copies, waits for them, and re-layouts  1.38 us

profile of v4, /device:TPU:1, one launch (start us, length us, event | category | flops | bytes accessed | tf_op | source)
XLA Modules:
  0.0 47.6 jit_solution(6095646239646856830)
XLA Ops:
  0.0 46.2 %shard_map.37 = bf16[32,512]{1,0:T(8,128)(2,1)} custom-call(s32[32]{0:T(128)} %lens_h.1, bf16[32,576]{1,0:T(8,128)(2,1)} %bitcast.5, bf16[32,32,8,576]{3,2,1,0:T(8,128)(2,1)} %bitcast.3), custom_call_target="tpu_custom_call" | custom-call | tf_op jit(solution)/shard_map/pallas_call | solution.py:381
  46.2 1.4 %copy.5 = bf16[32,1,512]{2,0,1:T(8,128)(2,1)} copy(bf16[32,1,512]{2,0,1:T(8,128)(2,1)} %bitcast.4) | data formatting | bytes 65536

commit v5 on v4

--- a/solution.py
+++ b/solution.py
@@ -41,21 +41,25 @@
     return [w * inv for w in ws], top + jnp.log2(tot)
 
 
-def _kernel(lens_h, q_h, c_h, o_h,
+def _kernel(lens_h, q_h, c_h, o_ref,
             lens, q_in, s1src, s1buf, q_even, q_odd, cbuf, obuf, lrow, wcol, r1d, r1l, r1m, lse1,
-            r2d, r2l, s3src, s3l, r3d, r3l, oout,
-            sem_l, sem_q, sem_o, c_s, c_r, s1_s, s1_r, s2_s, s2_r, s3_s, s3f_r, s3_r, sf_s,
+            r2d, r2l, s3src, s3l, r3d, r3l,
+            sem_l, sem_q, c_s, c_r, s1_s, s1_r, s2_s, s2_r, s3_s, s3f_r, s3_r, sf_s,
             r1_s, r1_r, r1l_s, r1l_r, r2_s, r2_r, r2l_s, r2l_r, r3_s, r3_r, r3l_s, r3l_r):
     d = lax.axis_index('dcp')
     core = d % 2
     co = ((d // 2) % 4, (d // 8) % 4, d // 32)
     partner = {'dcp': d + 1 - 2 * core}
 
+    nxt = (1, 2, 0)
+    ac = [co[n] + core * (co[nxt[n]] - co[n]) for n in KS]
+    stride = [STRIDE[n] + core * (STRIDE[nxt[n]] - STRIDE[n]) for n in KS]
+
     def ring(axis, off):
-        return {'dcp': d + ((co[axis] + off) % 4 - co[axis]) * STRIDE[axis]}
+        return {'dcp': d + ((ac[axis] + off) % 4 - ac[axis]) * stride[axis]}
 
     def line(axis, j):
-        return {'dcp': d + (j // 2 - co[axis]) * STRIDE[axis] + (j % 2 - core)}
+        return {'dcp': d + (j // 2 - ac[axis]) * stride[axis] + (j % 2 - core)}
 
     def send(src, dst, ss, rs, dev):
         pltpu.make_async_remote_copy(src_ref=src, dst_ref=dst, send_sem=ss, recv_sem=rs,
@@ -85,7 +89,8 @@
     for a in KS:
         for off in RING_OFFS:
             for c2 in DIRS:
-                pl.semaphore_signal(bar, inc=1, device_id=line(a, ((co[a] + off) % 4) * 2 + c2), device_id_type=MESH)
+                peer = d + ((co[a] + off) % 4 - co[a]) * STRIDE[a] + c2 - core
+                pl.semaphore_signal(bar, inc=1, device_id={'dcp': peer}, device_id_type=MESH)
     lrow[...] = jnp.zeros_like(lrow)
     load_l.wait()
 
@@ -99,13 +104,18 @@
     pl.semaphore_wait(bar, 19)
 
     def place(k):
-        return co[ORDERS[k][0]] * 2 + core
-
-    for k in KS:
+        return ac[ORDERS[k][0]] * 2 + core
+
+    for k in KS:
+        n = ORDERS[k][0]
         j0 = place(k)
-        for off in LINE_OFFS:
-            j = (j0 + off) % 8
-            send(s1src.at[j % 2, k], s1buf.at[k, j0], s1_s.at[k], s1_r.at[k], line(ORDERS[k][0], j))
+        oc = co[n] + co[nxt[n]] - ac[n]
+        ost = STRIDE[n] + STRIDE[nxt[n]] - stride[n]
+        for off in (2, 1, 3):
+            send(s1src.at[core, k], s1buf.at[k, j0], s1_s.at[k], s1_r.at[k], ring(n, off))
+        for off in (2, 1, 3, 0):
+            peer = {'dcp': d + ((oc + off) % 4 - oc) * ost + 1 - 2 * core}
+            send(s1src.at[1 - core, k], s1buf.at[k, oc * 2 + core], s1_s.at[k], s1_r.at[k], peer)
         s1buf[k, j0] = s1src[core, k]
     for i in range(NI):
         src, dst = cache_rows(i, 1 - core)
@@ -122,7 +132,7 @@
 
     def blk(k, i, off):
         _, a2, a3 = ORDERS[k]
-        return q_of(i).at[q_slot(k, i) + co[a3] * 4 + (co[a2] - off) % 4]
+        return q_of(i).at[q_slot(k, i) + ac[a3] * 4 + (ac[a2] - off) % 4]
 
     def copy3(k, i, off):
         b = blk(k, i, off)
@@ -146,8 +156,10 @@
             y = rows[8 * i:8 * i + 8, :LAT if i % 2 else QW]
             if i % 2 == 0:
                 y = jnp.concatenate([y, rows[8 * i + 8:8 * i + 16, LAT:]], axis=1)
-            q_of(i)[q_slot(k, i) + co[a3] * 4 + co[a2]] = y.astype(BF16)
-        for i in range(COUNT[k]):
+            q_of(i)[q_slot(k, i) + ac[a3] * 4 + ac[a2]] = y.astype(BF16)
+        stage2(k, 0)
+    for i in range(1, NI):
+        for k in ks_of(i):
             stage2(k, i)
 
     def stage3(i):
@@ -163,7 +175,7 @@
             for k in ks_of(i):
                 _, a2, a3 = ORDERS[k]
                 o = 1 if off < 2 else 3
-                b = q_of(i).at[q_slot(k, i) + ((co[a3] - o) % 4) * 4 + (co[a2] - off) % 4]
+                b = q_of(i).at[q_slot(k, i) + ((ac[a3] - o) % 4) * 4 + (ac[a2] - off) % 4]
                 send(b, b, sf_s.at[i % 2], s3_r.at[i], ring(a3, o))
 
     def arrive(i):
@@ -219,7 +231,7 @@
     def send1(k, i):
         a3 = ORDERS[k][2]
         for o in (2, 1, 3):
-            b = obuf.at[pl.ds(slot(k, i) + ((co[a3] + o) % 4) * 4, 4)]
+            b = obuf.at[pl.ds(slot(k, i) + ((ac[a3] + o) % 4) * 4, 4)]
             send(b, r1d.at[k, i, o - 1], r1_s, r1_r.at[wave(i), k], ring(a3, o))
 
     def members(w, k):
@@ -258,17 +270,17 @@
         ws, lse1[w, k] = _merge_weights([lrow[w, k]] + [r1l[w, k, x] for x in KS])
         for o in RING_OFFS:
             send(lse1.at[w, k], r2l.at[w, k, o - 1], r2l_s, r2l_r.at[w, k], ring(a2, o))
-        cols = columns(ws, co[a3] * 32, 32)
+        cols = columns(ws, ac[a3] * 32, 32)
         wait(obuf.at[pl.ds(0, 12 * len(its))], r1_r.at[w, k])
         for i in its:
-            y = obuf[pl.ds(slot(k, i) + co[a3] * 4, 4)].reshape(32, LAT).astype(F32) * cols(0, i - its[0])
+            y = obuf[pl.ds(slot(k, i) + ac[a3] * 4, 4)].reshape(32, LAT).astype(F32) * cols(0, i - its[0])
             for x in KS:
                 y = y + r1d[k, i, x].reshape(32, LAT).astype(F32) * cols(1 + x, i - its[0])
             y = y.astype(BF16).reshape(4, 8, LAT)
             for p in RING:
                 r1m[k, p, i] = y[p]
         for o in (2, 1, 3):
-            p = (co[a2] + o) % 4
+            p = (ac[a2] + o) % 4
             sl = pl.ds(its[0], len(its))
             send(r1m.at[k, p, sl], r2d.at[k, o - 1, sl], r2_s, r2_r.at[w, k], ring(a2, o))
 
@@ -279,18 +291,17 @@
         j0 = place(k)
         wait(r2l.at[w, k], r2l_r.at[w, k])
         ws, l2 = _merge_weights([lse1[w, k]] + [r2l[w, k, x] for x in KS])
-        g = co[a3] * 4 + co[a2]
+        g = ac[a3] * 4 + ac[a2]
         lt = pltpu.roll(l2, ((16 - g) % 16) * 8, 1)
+        s3l[w, k] = jnp.concatenate([lt] * 16, axis=0).T[0:8].reshape(8, 1, LANES)
         cols = columns(ws, g * 8, 8)
-        for j in range(8):
-            s3l[w, k, j] = jnp.broadcast_to(lt[:, j:j + 1], (8, LANES))
         for off in LINE_OFFS:
             j = (j0 + off) % 8
             send(s3l.at[w, k, j], r3l.at[w, k, j0], r3l_s, r3l_r.at[w, k], line(a1, j))
         wait(obuf.at[pl.ds(0, 3 * n)], r2_r.at[w, k])
         ys = []
         for i in its:
-            y = r1m[k, co[a2], i].astype(F32) * cols(0, i - its[0])
+            y = r1m[k, ac[a2], i].astype(F32) * cols(0, i - its[0])
             for x in KS:
                 y = y + r2d[k, x, i].astype(F32) * cols(1 + x, i - its[0])
             ys.append(y)
@@ -308,13 +319,14 @@
     def merge3(w, k):
         wait(r3l.at[w, k, pl.ds(0, 7)], r3l_r.at[w, k])
         wait(r3d.at[w, k, pl.ds(0, 7)], r3_r.at[w, k])
+        ls = [r3l[w, k, j] for j in range(8)]
+        ws = [None] * 8
         for h in DIRS:
-            ws, _ = _merge_weights([r3l[w, k, 2 * p + h] for p in RING])
-            y = None
-            for p in RING:
-                t = r3d[w, k, 2 * p + h].astype(F32) * jnp.concatenate([ws[p]] * 4, axis=1)
-                y = t if y is None else y + t
-            rows[w, h, k] = y
+            ws[h::2], _ = _merge_weights(ls[h::2])
+        cols = jnp.concatenate(ws, axis=0).T[0:8]
+        for h in DIRS:
+            ts = [r3d[w, k, j].astype(F32) * cols[:, j:j + 1] for j in range(h, 8, 2)]
+            rows[w, h, k] = functools.reduce(jnp.add, ts)
 
     for k in KS:
         merge1(0, k)
@@ -347,15 +359,12 @@
         s = 3 * (i + w * SPLIT) + k
         return (r == 16 * h + s) & (s < 16) & (i < SPLIT)
 
-    oout[...] = jnp.dot(_perm(32, 96, pick), flat, preferred_element_type=F32).astype(BF16)
-    store = pltpu.make_async_copy(oout, o_h, sem_o)
-    store.start()
+    o_ref[...] = jnp.dot(_perm(32, 96, pick), flat, preferred_element_type=F32).astype(BF16)
 
     for w in DIRS:
         for k in KS:
             wait(r3d.at[w, k, pl.ds(0, 7)], r3_s)
             wait(r3l.at[w, k, pl.ds(0, 7)], r3l_s)
-    store.wait()
 
 
 def solution(mesh):
@@ -371,22 +380,21 @@
             V((16, 64) + qtile, BF16), V((288,) + tile, BF16), V((2, 3) + row, F32), V((LANES, LANES), F32),
             V((3, NI, 3, 4) + tile, BF16), V((2, 3, 3) + row, F32), V((3, 4, NI) + tile, BF16), V((2, 3) + row, F32),
             V((3, 3, NI) + tile, BF16), V((2, 3, 3) + row, F32),
-            V(line + tile, BF16), V(line + row, F32), V(line + tile, BF16), V(line + row, F32),
-            V((32, LAT), BF16),
-            dma, dma, dma, dma, dma((NI,)), dma((3,)), dma((3,)), dma((2,)), dma((NI,)),
+            V(line + tile, BF16), V(line + (1, LANES), F32), V(line + tile, BF16), V(line + (1, LANES), F32),
+            dma, dma, dma, dma((NI,)), dma((3,)), dma((3,)), dma((2,)), dma((NI,)),
             dma((2,)), dma((NI,)), dma((NI,)), dma((2,)),
             dma, dma((2, 3)), dma, dma((2, 3)), dma, dma((2, 3)), dma, dma((2, 3)),
             dma, dma((2, 3)), dma, dma((2, 3)),
         ]
         o = pl.pallas_call(
             _kernel,
-            out_shape=jax.ShapeDtypeStruct((32, LAT), BF16),
+            out_shape=V((32, LAT), BF16),
             in_specs=[anyspace] * 3,
-            out_specs=anyspace,
+            out_specs=pl.BlockSpec(memory_space=V),
             scratch_shapes=scratch,
             compiler_params=pltpu.CompilerParams(collective_id=0, has_side_effects=True,
-                                                 vmem_limit_bytes=58 * 2 ** 20),
-        )(lens, q.reshape(32, QW), cache.reshape(32, 32, 8, QW))
+                                                 vmem_limit_bytes=50 * 2 ** 20),
+        )(*[pltpu.with_memory_space_constraint(v, pltpu.HBM) for v in (lens, q.reshape(32, QW), cache.reshape(32, 32, 8, QW))])
         return o.reshape(32, 1, LAT)
 
     return jax.shard_map(local, mesh=mesh,

time: 47.7 us -> 45.2 us (0.948)
  Pallas kernels: 46.2 us -> 44.4 us
  local copies, waits for them, and re-layouts: 1.38 us -> 0.62 us
    pallas_call x1, Pallas kernels: 46.2 us -> 44.4 us  [local(): pl.pallas_call(_kernel, out_shape=V((32, LAT), BF16), in_specs=[anyspace]...]
    unnamed x1, local copies, waits for them, and re-layouts: 1.38 us -> 0.62 us
where the time goes in v5:
time: 45.2 us; the launch traced here: 45.1 us
  Pallas kernels  44.4 us (98%)
  local copies, waits for them, and re-layouts  0.62 us (1%)
    pallas_call x1, Pallas kernels, local(): pl.pallas_call(_kernel, out_shape=V((32, LAT), BF16), in_specs=[anyspace]...  44.4 us

profile of v5, /device:TPU:1, one launch (start us, length us, event | category | flops | bytes accessed | tf_op | source)
XLA Modules:
  0.0 45.1 jit_solution(4969534692989526802)
XLA Ops:
  0.0 44.4 %shard_map.37 = bf16[32,512]{1,0:T(8,128)(2,1)S(1)} custom-call(s32[32]{0:T(128)} %lens_h.1, bf16[32,576]{1,0:T(8,128)(2,1)} %bitcast.5, bf16[32,32,8,576]{3,2,1,0:T(8,128)(2,1)} %bitcast.4), custom_call_target="tpu_custom_call" | custom-call | tf_op jit(solution)/shard_map/pallas_call | solution.py:389
  44.4 0.6 %copy.5 = bf16[32,1,512]{2,0,1:T(8,128)(2,1)} copy(bf16[32,1,512]{2,0,1:T(8,128)(2,1)S(1)} %bitcast.3) | data formatting | bytes 65536

commit v6 on v5

v6 whole, which is shorter than its diff:
```python
import functools
import math

import jax
import jax.numpy as jnp
from jax import lax
from jax.experimental import pallas as pl
from jax.experimental.pallas import tpu as pltpu
from jax.sharding import PartitionSpec as P

ROPE = 64
QK_DIM = 192
SCALE2 = QK_DIM ** -0.5 * math.log2(math.e)
NEG = -3.0e38
MESH = pl.DeviceIdType.MESH
F32 = jnp.float32
BF16 = jnp.bfloat16

STRIDE = (2, 8, 32)
ORDERS = ((0, 1, 2), (1, 2, 0), (2, 0, 1))
COUNT = (6, 5, 5)
NI = 6
SPLIT = 3


LAT, QW, LANES = 512, 576, 128
KS, DIRS, RING, RING_OFFS, LINE_OFFS = range(3), range(2), range(4), range(1, 4), range(1, 8)


def _perm(rows, cols, f):
    r = lax.broadcasted_iota(jnp.int32, (rows, cols), 0)
    c = lax.broadcasted_iota(jnp.int32, (rows, cols), 1)
    return f(r, c).astype(F32).astype(BF16)


def _merge_weights(lses):
    top = functools.reduce(jnp.maximum, lses)
    ws = [jnp.exp2(v - top) for v in lses]
    tot = functools.reduce(jnp.add, ws)
    inv = 1.0 / tot
    return [w * inv for w in ws], top + jnp.log2(tot)


def _kernel(lens_h, q_h, c_h, o_ref,
            lens, q_in, s1src, s1buf, q_even, q_odd, cbuf, obuf, lrow, wcol, r1d, r1l, r1m, lse1,
            r2d, r2l, s3src, s3l, r3d, r3l,
            sem_l, sem_q, c_s, c_r, s1_s, s1_r, s2_s, s2_r, s3_s, s3_r,
            r1_s, r1_r, r1l_s, r1l_r, r2_s, r2_r, r2l_s, r2l_r, r3_s, r3_r, r3l_s, r3l_r):
    d = lax.axis_index('dcp')
    core = d % 2
    co = ((d // 2) % 4, (d // 8) % 4, d // 32)
    partner = {'dcp': d + 1 - 2 * core}

    nxt = (1, 2, 0)
    ac = [co[n] + core * (co[nxt[n]] - co[n]) for n in KS]
    stride = [STRIDE[n] + core * (STRIDE[nxt[n]] - STRIDE[n]) for n in KS]

    def ring(axis, off):
        return {'dcp': d + ((ac[axis] + off) % 4 - ac[axis]) * stride[axis]}

    def line(axis, j):
        return {'dcp': d + (j // 2 - ac[axis]) * stride[axis] + (j % 2 - core)}

    def send(src, dst, ss, rs, dev):
        pltpu.make_async_remote_copy(src_ref=src, dst_ref=dst, send_sem=ss, recv_sem=rs,
                                     device_id=dev, device_id_type=MESH).start()

    def wait(ref, sem):
        pltpu.make_async_copy(ref, ref, sem).wait()

    def ks_of(i):
        return KS if i < NI - 1 else range(1)

    load_q = pltpu.make_async_copy(q_h, q_in, sem_q)
    load_q.start()
    load_l = pltpu.make_async_copy(lens_h, lens, sem_l)
    load_l.start()

    def cache_rows(i, half):
        n = len(ks_of(i))
        return c_h.at[pl.ds(16 * half + 3 * i, n)], cbuf.at[pl.ds(3 * i, n), pl.ds(32 * core, 32)]

    for i in range(NI):
        src, dst = cache_rows(i, core)
        pltpu.make_async_copy(src, dst, c_r).start()

    bar = pltpu.get_barrier_semaphore()
    pl.semaphore_signal(bar, inc=1, device_id=partner, device_id_type=MESH)
    for a in KS:
        for off in RING_OFFS:
            for c2 in DIRS:
                peer = d + ((co[a] + off) % 4 - co[a]) * STRIDE[a] + c2 - core
                pl.semaphore_signal(bar, inc=1, device_id={'dcp': peer}, device_id_type=MESH)
    lrow[...] = jnp.zeros_like(lrow)
    load_l.wait()

    def sel(r, c):
        s = 3 * (r % 8) + (r // 8) % 3
        return (c == 16 * (r // 24) + s) & (s < 16)

    load_q.wait()
    qp = jnp.dot(_perm(48, 32, sel), q_in[...], preferred_element_type=F32).astype(BF16)
    s1src[...] = qp.reshape(2, 3, 8, QW)
    pl.semaphore_wait(bar, 19)

    def place(k):
        return ac[ORDERS[k][0]] * 2 + core

    for k in KS:
        n = ORDERS[k][0]
        j0 = place(k)
        oc = co[n] + co[nxt[n]] - ac[n]
        ost = STRIDE[n] + STRIDE[nxt[n]] - stride[n]
        for off in (2, 1, 3):
            send(s1src.at[core, k], s1buf.at[k, j0], s1_s, s1_r, ring(n, off))
        for off in (2, 1, 3, 0):
            peer = {'dcp': d + ((oc + off) % 4 - oc) * ost + 1 - 2 * core}
            send(s1src.at[1 - core, k], s1buf.at[k, oc * 2 + core], s1_s, s1_r, peer)
        s1buf[k, j0] = s1src[core, k]
    for i in range(NI):
        src, dst = cache_rows(i, 1 - core)
        send(src, dst, c_s, c_r, partner)

    def q_of(i):
        return q_odd if i % 2 else q_even

    def q_slot(k, i):
        return (k * 3 + i // 2) * 16

    def slot(k, i):
        return (k * NI + i) * 16

    def blk(k, i, off):
        _, a2, a3 = ORDERS[k]
        return q_of(i).at[q_slot(k, i) + ac[a3] * 4 + (ac[a2] - off) % 4]

    def copy3(k, i, off):
        b = blk(k, i, off)
        a3 = ORDERS[k][2]
        for o in (2, 1, 3):
            send(b, b, s3_s.at[i % 2], s3_r.at[i], ring(a3, o))

    def stage2(k, i):
        b = blk(k, i, 0)
        for off in (2, 1, 3):
            send(b, b, s2_s.at[i % 2], s2_r.at[i], ring(ORDERS[k][1], off))
        copy3(k, i, 0)

    tr = _perm(64, 64, lambda r, c: (r // 8 == c % 8) & (r % 8 == c // 8))
    wait(s1buf.at[:, pl.ds(0, 7)], s1_r)
    turned = [jnp.dot(tr, s1buf[k].reshape(64, QW), preferred_element_type=F32) for k in KS]
    for k in KS:
        rows = turned[k]
        _, a2, a3 = ORDERS[k]
        for i in range(COUNT[k]):
            y = rows[8 * i:8 * i + 8, :LAT if i % 2 else QW]
            if i % 2 == 0:
                y = jnp.concatenate([y, rows[8 * i + 8:8 * i + 16, LAT:]], axis=1)
            q_of(i)[q_slot(k, i) + ac[a3] * 4 + ac[a2]] = y.astype(BF16)
    for i in range(NI):
        for k in ks_of(i):
            stage2(k, i)

    def stage3(i):
        n = len(ks_of(i))
        wait(q_of(i).at[pl.ds(0, 3 * n)], s2_r.at[i])
        for off in (1, 3, 2):
            for k in ks_of(i):
                copy3(k, i, off)

    def arrive(i):
        n = len(ks_of(i))
        if i == 0:
            wait(cbuf, c_r)
        wait(q_of(i).at[pl.ds(0, 12 * n)], s3_r.at[i])

    for i in range(NI):
        stage3(i)

    chip8 = (d // 2) * 16

    j = lax.broadcasted_iota(jnp.int32, (LAT, LANES), 0)
    pos = (j & 7) + ((j >> 3) & 31) * 1024 + (j >> 8) * 8

    def cache_of(k, i):
        return cbuf[3 * i + k].reshape(LAT, QW)

    def scores(k, i):
        cs = cache_of(k, i)
        n = pl.ds(q_slot(k, i), 16)
        lat = q_of(i)[n, :, :LAT].reshape(LANES, LAT)
        rope = q_even[n, :, LAT:].reshape(LANES, LANES)
        rope = rope[:, ROPE:] if i % 2 else rope[:, :ROPE]
        dims = (((1,), (1,)), ((), ()))
        st = lax.dot_general(cs[:, :LAT], lat, dims, preferred_element_type=F32)
        return (st + lax.dot_general(cs[:, LAT:], rope, dims, preferred_element_type=F32)) * SCALE2

    def softmax(st, k, i):
        ok = pos < lens[16 * core + 3 * i + k] - chip8
        st = jnp.where(ok, st, NEG)
        m = jnp.max(st, axis=0, keepdims=True)
        p = jnp.where(ok, jnp.exp2(st - m), 0.0)
        l = jnp.sum(p, axis=0, keepdims=True)
        has = l > 0.0
        ls = jnp.where(has, l, 1.0)
        w = wave(i)
        lrow[w, k, i - w * SPLIT:i - w * SPLIT + 1, :] = jnp.where(has, m + jnp.log2(ls), NEG)
        return (p * (1.0 / ls)).astype(BF16)

    def attend(i):
        ks = ks_of(i)
        sts = [scores(k, i) for k in ks]
        ps = [softmax(st, k, i) for st, k in zip(sts, ks)]
        outs = [lax.dot_general(p, cache_of(k, i)[:, :LAT], (((0,), (0,)), ((), ())), preferred_element_type=F32)
                for p, k in zip(ps, ks)]
        for o, k in zip(outs, ks):
            obuf[pl.ds(slot(k, i), 16)] = o.astype(BF16).reshape(16, 8, LAT)

    def wave(i):
        return 0 if i < SPLIT else 1

    def send1(k, i):
        a3 = ORDERS[k][2]
        for o in (2, 1, 3):
            b = obuf.at[pl.ds(slot(k, i) + ((ac[a3] + o) % 4) * 4, 4)]
            send(b, r1d.at[k, i, o - 1], r1_s, r1_r.at[wave(i)], ring(a3, o))

    def members(w, k):
        return range(SPLIT) if w == 0 else range(SPLIT, COUNT[k])

    def count(w):
        return sum(len(members(w, k)) for k in KS)

    def send1_lse(w):
        for k in KS:
            for o in RING_OFFS:
                send(lrow.at[w, k], r1l.at[w, k, o - 1], r1l_s, r1l_r.at[w], ring(ORDERS[k][2], o))

    for i in range(NI):
        with jax.named_scope(f"arrive{i}"):
            arrive(i)
        with jax.named_scope(f"attend{i}"):
            attend(i)
            if i == NI - 1:
                send1_lse(1)
            for k in ks_of(i):
                send1(k, i)
        with jax.named_scope(f"rest{i}"):
            if i == SPLIT - 1:
                send1_lse(0)


    def columns(ws, k, row, n):
        wcol[k, :, :32] = jnp.concatenate(ws, axis=0).T
        t = wcol[k, pl.ds(row, n), :32]
        return lambda x, i: t[:, 8 * x + i:8 * x + i + 1]

    def weighted(cols, i, parts):
        return functools.reduce(jnp.add, [p.astype(F32) * cols(x, i) for x, p in enumerate(parts)])

    def merge1(w):
        cols = []
        wait(r1l.at[w], r1l_r.at[w])
        for k in KS:
            ws, lse1[w, k] = _merge_weights([lrow[w, k]] + [r1l[w, k, x] for x in KS])
            cols.append(columns(ws, k, ac[ORDERS[k][2]] * 32, 32))
        for k in KS:
            for o in RING_OFFS:
                send(lse1.at[w, k], r2l.at[w, k, o - 1], r2l_s, r2l_r.at[w], ring(ORDERS[k][1], o))
        wait(obuf.at[pl.ds(0, 12 * count(w))], r1_r.at[w])
        for k in KS:
            _, a2, a3 = ORDERS[k]
            its = members(w, k)
            for i in its:
                own = obuf[pl.ds(slot(k, i) + ac[a3] * 4, 4)]
                parts = [v.reshape(32, LAT) for v in [own] + [r1d[k, i, x] for x in KS]]
                y = weighted(cols[k], i - its[0], parts).astype(BF16).reshape(4, 8, LAT)
                for p in RING:
                    r1m[k, p, i] = y[p]
            for o in (2, 1, 3):
                sl = pl.ds(its[0], len(its))
                send(r1m.at[k, (ac[a2] + o) % 4, sl], r2d.at[k, o - 1, sl], r2_s, r2_r.at[w], ring(a2, o))

    def merge2(w):
        cols = []
        wait(r2l.at[w], r2l_r.at[w])
        for k in KS:
            _, a2, a3 = ORDERS[k]
            ws, l2 = _merge_weights([lse1[w, k]] + [r2l[w, k, x] for x in KS])
            g = ac[a3] * 4 + ac[a2]
            lt = pltpu.roll(l2, ((16 - g) % 16) * 8, 1)
            s3l[w, k] = jnp.concatenate([lt] * 16, axis=0).T[0:8].reshape(8, 1, LANES)
            cols.append(columns(ws, k, g * 8, 8))
        for k in KS:
            j0 = place(k)
            for off in LINE_OFFS:
                j = (j0 + off) % 8
                send(s3l.at[w, k, j], r3l.at[w, k, j0], r3l_s, r3l_r.at[w], line(ORDERS[k][0], j))
            r3l[w, k, j0] = s3l[w, k, j0]
        wait(obuf.at[pl.ds(0, 3 * count(w))], r2_r.at[w])
        tiles = []
        for k in KS:
            its = members(w, k)
            ys = [weighted(cols[k], i - its[0], [r1m[k, ac[ORDERS[k][1]], i]] + [r2d[k, x, i] for x in KS]) for i in its]
            n = len(its)
            pm = _perm(64, 8 * n, lambda r, c: (c == (r % 8) * 8 + r // 8) & (r % 8 < n))
            tiles.append(jnp.dot(pm, jnp.concatenate(ys, axis=0).astype(BF16), preferred_element_type=F32))
        for k in KS:
            s3src[w, k] = tiles[k].astype(BF16).reshape(8, 8, LAT)
            j0 = place(k)
            for off in (3, 4, 5, 2, 6, 1, 7):
                j = (j0 + off) % 8
                send(s3src.at[w, k, j], r3d.at[w, k, j0], r3_s, r3_r.at[w], line(ORDERS[k][0], j))
            r3d[w, k, j0] = s3src[w, k, j0]

    rows = {}

    def merge3(w):
        cols = []
        wait(r3l.at[w, :, pl.ds(0, 7)], r3l_r.at[w])
        for k in KS:
            ls = [r3l[w, k, j] for j in range(8)]
            ws = [None] * 8
            for h in DIRS:
                ws[h::2], _ = _merge_weights(ls[h::2])
            cols.append(jnp.concatenate(ws, axis=0).T[0:8])
        wait(r3d.at[w, :, pl.ds(0, 7)], r3_r.at[w])
        for k in KS:
            for h in DIRS:
                ts = [r3d[w, k, j].astype(F32) * cols[k][:, j:j + 1] for j in range(h, 8, 2)]
                rows[w, h, k] = functools.reduce(jnp.add, ts)

    merge1(0)
    merge1(1)
    merge2(0)
    wait(s1buf.at[:, pl.ds(0, 7)], s1_s)
    wait(cbuf.at[pl.ds(0, 8)], c_s)
    for par in DIRS:
        its = [i for i in range(NI) for _ in ks_of(i) if i % 2 == par]
        wait(q_of(par).at[pl.ds(0, 3 * len(its))], s2_s.at[par])
        wait(q_of(par).at[pl.ds(0, 12 * len(its))], s3_s.at[par])
    merge2(1)
    merge3(0)
    wait(obuf.at[pl.ds(0, 192)], r1_s)
    wait(r1l, r1l_s)
    wait(obuf.at[pl.ds(0, 48)], r2_s)
    wait(r2l, r2l_s)
    merge3(1)
    flat = jnp.concatenate([rows[w, h, k] for w in DIRS for h in DIRS for k in KS], axis=0).astype(BF16)

    def pick(r, c):
        w, h, k, i = c // 48, (c // 24) % 2, (c // 8) % 3, c % 8
        s = 3 * (i + w * SPLIT) + k
        return (r == 16 * h + s) & (s < 16) & (i < SPLIT)

    o_ref[...] = jnp.dot(_perm(32, 96, pick), flat, preferred_element_type=F32).astype(BF16)

    wait(r3d.at[:, :, pl.ds(0, 7)], r3_s)
    wait(r3l.at[:, :, pl.ds(0, 7)], r3l_s)


def solution(mesh):
    def local(q, cache, lens):
        dma = pltpu.SemaphoreType.DMA
        V = pltpu.VMEM
        anyspace = pl.BlockSpec(memory_space=pl.ANY)
        tile, qtile, row = (8, LAT), (8, QW), (8, LANES)
        line = (2, 3, 8)
        scratch = [
            pltpu.SMEM((32,), jnp.int32), V((32, QW), BF16), V((2, 3) + qtile, BF16), V((3, 8) + qtile, BF16),
            V((144, 8, LAT + LANES), BF16), V((144,) + tile, BF16),
            V((16, 64) + qtile, BF16), V((288,) + tile, BF16), V((2, 3) + row, F32), V((3, LANES, LANES), F32),
            V((3, NI, 3, 4) + tile, BF16), V((2, 3, 3) + row, F32), V((3, 4, NI) + tile, BF16), V((2, 3) + row, F32),
            V((3, 3, NI) + tile, BF16), V((2, 3, 3) + row, F32),
            V(line + tile, BF16), V(line + (1, LANES), F32), V(line + tile, BF16), V(line + (1, LANES), F32),
            dma, dma, dma, dma, dma, dma, dma((2,)), dma((NI,)), dma((2,)), dma((NI,)),
            dma, dma((2,)), dma, dma((2,)), dma, dma((2,)), dma, dma((2,)), dma, dma((2,)), dma, dma((2,)),
        ]
        o = pl.pallas_call(
            _kernel,
            out_shape=V((32, LAT), BF16),
            in_specs=[anyspace] * 3,
            out_specs=pl.BlockSpec(memory_space=V),
            scratch_shapes=scratch,
            compiler_params=pltpu.CompilerParams(collective_id=0, has_side_effects=True,
                                                 vmem_limit_bytes=50 * 2 ** 20),
        )(*[pltpu.with_memory_space_constraint(v, pltpu.HBM) for v in (lens, q.reshape(32, QW), cache.reshape(32, 32, 8, QW))])
        return o.reshape(32, 1, LAT)

    return jax.shard_map(local, mesh=mesh,
                         in_specs=(P('dp', 'dcp', None), P('dp', None, 'dcp', None, None), P('dp')),
                         out_specs=P('dp', 'dcp', None), check_vma=False)
```

time: 45.2 us -> 42.9 us (0.949)
  Pallas kernels: 44.4 us -> 42.2 us
    pallas_call x1, Pallas kernels: 44.4 us -> 42.2 us  [local(): pl.pallas_call(_kernel, out_shape=V((32, LAT), BF16), in_specs=[anyspace]...]
where the time goes in v6:
time: 42.9 us; the launch traced here: 42.8 us
  Pallas kernels  42.2 us (98%)
  local copies, waits for them, and re-layouts  0.62 us (1%)
    pallas_call x1, Pallas kernels, local(): pl.pallas_call(_kernel, out_shape=V((32, LAT), BF16), in_specs=[anyspace]...  42.2 us

profile of v6, /device:TPU:1, one launch (start us, length us, event | category | flops | bytes accessed | tf_op | source)
XLA Modules:
  0.0 42.8 jit_solution(12942183050530193425)
XLA Ops:
  0.0 42.2 %shard_map.37 = bf16[32,512]{1,0:T(8,128)(2,1)S(1)} custom-call(s32[32]{0:T(128)} %lens_h.1, bf16[32,576]{1,0:T(8,128)(2,1)} %bitcast.5, bf16[32,32,8,576]{3,2,1,0:T(8,128)(2,1)} %bitcast.4), custom_call_target="tpu_custom_call" | custom-call | tf_op jit(solution)/shard_map/pallas_call | solution.py:379
  42.2 0.6 %copy.5 = bf16[32,1,512]{2,0,1:T(8,128)(2,1)} copy(bf16[32,1,512]{2,0,1:T(8,128)(2,1)S(1)} %bitcast.3) | data formatting | bytes 65536

commit v7 on v6

--- a/solution.py
+++ b/solution.py
@@ -21,6 +21,7 @@
 COUNT = (6, 5, 5)
 NI = 6
 SPLIT = 3
+ORDER, RELAYED = (0, 3, 4, 5, 1, 2), (3, 4, 5)
 
 
 LAT, QW, LANES = 512, 576, 128
@@ -44,7 +45,7 @@
 def _kernel(lens_h, q_h, c_h, o_ref,
             lens, q_in, s1src, s1buf, q_even, q_odd, cbuf, obuf, lrow, wcol, r1d, r1l, r1m, lse1,
             r2d, r2l, s3src, s3l, r3d, r3l,
-            sem_l, sem_q, c_s, c_r, s1_s, s1_r, s2_s, s2_r, s3_s, s3_r,
+            sem_l, sem_q, c_s, c_r, s1_s, s1_r, s2_s, s2_r, s3_s, s3_r, sf_r,
             r1_s, r1_r, r1l_s, r1l_r, r2_s, r2_r, r2l_s, r2l_r, r3_s, r3_r, r3l_s, r3l_r):
     d = lax.axis_index('dcp')
     core = d % 2
@@ -70,19 +71,6 @@
 
     def ks_of(i):
         return KS if i < NI - 1 else range(1)
-
-    load_q = pltpu.make_async_copy(q_h, q_in, sem_q)
-    load_q.start()
-    load_l = pltpu.make_async_copy(lens_h, lens, sem_l)
-    load_l.start()
-
-    def cache_rows(i, half):
-        n = len(ks_of(i))
-        return c_h.at[pl.ds(16 * half + 3 * i, n)], cbuf.at[pl.ds(3 * i, n), pl.ds(32 * core, 32)]
-
-    for i in range(NI):
-        src, dst = cache_rows(i, core)
-        pltpu.make_async_copy(src, dst, c_r).start()
 
     bar = pltpu.get_barrier_semaphore()
     pl.semaphore_signal(bar, inc=1, device_id=partner, device_id_type=MESH)
@@ -91,6 +79,19 @@
             for c2 in DIRS:
                 peer = d + ((co[a] + off) % 4 - co[a]) * STRIDE[a] + c2 - core
                 pl.semaphore_signal(bar, inc=1, device_id={'dcp': peer}, device_id_type=MESH)
+    load_q = pltpu.make_async_copy(q_h, q_in, sem_q)
+    load_q.start()
+    load_l = pltpu.make_async_copy(lens_h, lens, sem_l)
+    load_l.start()
+
+    def cache_rows(i, half):
+        n = len(ks_of(i))
+        return c_h.at[pl.ds(16 * half + 3 * i, n)], cbuf.at[pl.ds(3 * i, n), pl.ds(32 * core, 32)]
+
+    for i in range(NI):
+        src, dst = cache_rows(i, core)
+        pltpu.make_async_copy(src, dst, c_r).start()
+
     lrow[...] = jnp.zeros_like(lrow)
     load_l.wait()
 
@@ -137,8 +138,9 @@
     def copy3(k, i, off):
         b = blk(k, i, off)
         a3 = ORDERS[k][2]
-        for o in (2, 1, 3):
-            send(b, b, s3_s.at[i % 2], s3_r.at[i], ring(a3, o))
+        for o in (1, 3) if i in RELAYED else (2, 1, 3):
+            onward = i in RELAYED and off // 2 == o // 2
+            send(b, b, s3_s.at[i % 2], sf_r.at[i] if onward else s3_r.at[i], ring(a3, o))
 
     def stage2(k, i):
         b = blk(k, i, 0)
@@ -157,7 +159,7 @@
             if i % 2 == 0:
                 y = jnp.concatenate([y, rows[8 * i + 8:8 * i + 16, LAT:]], axis=1)
             q_of(i)[q_slot(k, i) + ac[a3] * 4 + ac[a2]] = y.astype(BF16)
-    for i in range(NI):
+    for i in ORDER:
         for k in ks_of(i):
             stage2(k, i)
 
@@ -168,13 +170,22 @@
             for k in ks_of(i):
                 copy3(k, i, off)
 
+    def forward(i):
+        wait(q_of(i).at[pl.ds(0, 4 * len(ks_of(i)))], sf_r.at[i])
+        for off in RING:
+            for k in ks_of(i):
+                _, a2, a3 = ORDERS[k]
+                o = 1 if off < 2 else 3
+                b = q_of(i).at[q_slot(k, i) + ((ac[a3] - o) % 4) * 4 + (ac[a2] - off) % 4]
+                send(b, b, s3_s.at[i % 2], s3_r.at[i], ring(a3, o))
+
     def arrive(i):
         n = len(ks_of(i))
         if i == 0:
             wait(cbuf, c_r)
-        wait(q_of(i).at[pl.ds(0, 12 * n)], s3_r.at[i])
-
-    for i in range(NI):
+        wait(q_of(i).at[pl.ds(0, (8 if i in RELAYED else 12) * n)], s3_r.at[i])
+
+    for i in ORDER:
         stage3(i)
 
     chip8 = (d // 2) * 16
@@ -199,21 +210,19 @@
         ok = pos < lens[16 * core + 3 * i + k] - chip8
         st = jnp.where(ok, st, NEG)
         m = jnp.max(st, axis=0, keepdims=True)
-        p = jnp.where(ok, jnp.exp2(st - m), 0.0)
-        l = jnp.sum(p, axis=0, keepdims=True)
-        has = l > 0.0
-        ls = jnp.where(has, l, 1.0)
+        has = m > NEG
+        p = jnp.exp2(st - jnp.where(has, m, 0.0))
+        ls = jnp.where(has, jnp.sum(p, axis=0, keepdims=True), 1.0)
         w = wave(i)
         lrow[w, k, i - w * SPLIT:i - w * SPLIT + 1, :] = jnp.where(has, m + jnp.log2(ls), NEG)
         return (p * (1.0 / ls)).astype(BF16)
 
-    def attend(i):
-        ks = ks_of(i)
-        sts = [scores(k, i) for k in ks]
-        ps = [softmax(st, k, i) for st, k in zip(sts, ks)]
+    def attend(batch):
+        sts = [scores(k, i) for k, i in batch]
+        ps = [softmax(st, k, i) for st, (k, i) in zip(sts, batch)]
         outs = [lax.dot_general(p, cache_of(k, i)[:, :LAT], (((0,), (0,)), ((), ())), preferred_element_type=F32)
-                for p, k in zip(ps, ks)]
-        for o, k in zip(outs, ks):
+                for p, (k, i) in zip(ps, batch)]
+        for o, (k, i) in zip(outs, batch):
             obuf[pl.ds(slot(k, i), 16)] = o.astype(BF16).reshape(16, 8, LAT)
 
     def wave(i):
@@ -236,18 +245,25 @@
             for o in RING_OFFS:
                 send(lrow.at[w, k], r1l.at[w, k, o - 1], r1l_s, r1l_r.at[w], ring(ORDERS[k][2], o))
 
-    for i in range(NI):
+    for i in range(NI - 1):
+        batch = [(k, i) for k in KS]
         with jax.named_scope(f"arrive{i}"):
             arrive(i)
+            if i == NI - 2:
+                arrive(i + 1)
+                batch.append((0, i + 1))
         with jax.named_scope(f"attend{i}"):
-            attend(i)
-            if i == NI - 1:
-                send1_lse(1)
-            for k in ks_of(i):
-                send1(k, i)
+            attend(batch)
         with jax.named_scope(f"rest{i}"):
+            if i == 0:
+                for x in RELAYED:
+                    forward(x)
             if i == SPLIT - 1:
                 send1_lse(0)
+            if i == NI - 2:
+                send1_lse(1)
+            for k, x in batch:
+                send1(k, x)
 
 
     def columns(ws, k, row, n):
@@ -373,7 +389,7 @@
             V((3, NI, 3, 4) + tile, BF16), V((2, 3, 3) + row, F32), V((3, 4, NI) + tile, BF16), V((2, 3) + row, F32),
             V((3, 3, NI) + tile, BF16), V((2, 3, 3) + row, F32),
             V(line + tile, BF16), V(line + (1, LANES), F32), V(line + tile, BF16), V(line + (1, LANES), F32),
-            dma, dma, dma, dma, dma, dma, dma((2,)), dma((NI,)), dma((2,)), dma((NI,)),
+            dma, dma, dma, dma, dma, dma, dma((2,)), dma((NI,)), dma((2,)), dma((NI,)), dma((NI,)),
             dma, dma((2,)), dma, dma((2,)), dma, dma((2,)), dma, dma((2,)), dma, dma((2,)), dma, dma((2,)),
         ]
         o = pl.pallas_call(

time: 42.9 us -> 42.9 us (level)
  no operation moved by 1% of the time
where the time goes in v7:
time: 42.9 us; the launch traced here: 42.8 us
  Pallas kernels  42.2 us (98%)
  local copies, waits for them, and re-layouts  0.62 us (1%)
    pallas_call x1, Pallas kernels, local(): pl.pallas_call(_kernel, out_shape=V((32, LAT), BF16), in_specs=[anyspace]...  42.2 us

profile of v7, /device:TPU:1, one launch (start us, length us, event | category | flops | bytes accessed | tf_op | source)
XLA Modules:
  0.0 42.8 jit_solution(15971455686755816413)
XLA Ops:
  0.0 42.2 %shard_map.37 = bf16[32,512]{1,0:T(8,128)(2,1)S(1)} custom-call(s32[32]{0:T(128)} %lens_h.1, bf16[32,576]{1,0:T(8,128)(2,1)} %bitcast.5, bf16[32,32,8,576]{3,2,1,0:T(8,128)(2,1)} %bitcast.4), custom_call_target="tpu_custom_call" | custom-call | tf_op jit(solution)/shard_map/pallas_call | solution.py:395
  42.2 0.6 %copy.5 = bf16[32,1,512]{2,0,1:T(8,128)(2,1)} copy(bf16[32,1,512]{2,0,1:T(8,128)(2,1)S(1)} %bitcast.3) | data formatting | bytes 65536

commit v8 on v7

--- a/solution.py
+++ b/solution.py
@@ -20,7 +20,8 @@
 ORDERS = ((0, 1, 2), (1, 2, 0), (2, 0, 1))
 COUNT = (6, 5, 5)
 NI = 6
-SPLIT = 3
+SPLIT = 4
+TILE = (SPLIT, NI - SPLIT)
 ORDER, RELAYED = (0, 3, 4, 5, 1, 2), (3, 4, 5)
 
 
@@ -44,7 +45,7 @@
 
 def _kernel(lens_h, q_h, c_h, o_ref,
             lens, q_in, s1src, s1buf, q_even, q_odd, cbuf, obuf, lrow, wcol, r1d, r1l, r1m, lse1,
-            r2d, r2l, s3src, s3l, r3d, r3l,
+            r2d, r2l, s3a, s3b, s3l, r3a, r3b, r3l, fin,
             sem_l, sem_q, c_s, c_r, s1_s, s1_r, s2_s, s2_r, s3_s, s3_r, sf_r,
             r1_s, r1_r, r1l_s, r1l_r, r2_s, r2_r, r2l_s, r2l_r, r3_s, r3_r, r3l_s, r3l_r):
     d = lax.axis_index('dcp')
@@ -93,6 +94,7 @@
         pltpu.make_async_copy(src, dst, c_r).start()
 
     lrow[...] = jnp.zeros_like(lrow)
+    fin[...] = jnp.zeros_like(fin)
     load_l.wait()
 
     def sel(r, c):
@@ -214,7 +216,7 @@
         p = jnp.exp2(st - jnp.where(has, m, 0.0))
         ls = jnp.where(has, jnp.sum(p, axis=0, keepdims=True), 1.0)
         w = wave(i)
-        lrow[w, k, i - w * SPLIT:i - w * SPLIT + 1, :] = jnp.where(has, m + jnp.log2(ls), NEG)
+        lrow[w, k, i - w * SPLIT] = jnp.where(has, m + jnp.log2(ls), NEG)
         return (p * (1.0 / ls)).astype(BF16)
 
     def attend(batch):
@@ -243,7 +245,8 @@
     def send1_lse(w):
         for k in KS:
             for o in RING_OFFS:
-                send(lrow.at[w, k], r1l.at[w, k, o - 1], r1l_s, r1l_r.at[w], ring(ORDERS[k][2], o))
+                n = pl.ds(0, TILE[w])
+                send(lrow.at[w, k, n], r1l.at[w, k, o - 1, n], r1l_s.at[w], r1l_r.at[w], ring(ORDERS[k][2], o))
 
     for i in range(NI - 1):
         batch = [(k, i) for k in KS]
@@ -274,15 +277,21 @@
     def weighted(cols, i, parts):
         return functools.reduce(jnp.add, [p.astype(F32) * cols(x, i) for x, p in enumerate(parts)])
 
+    def tile_of(w, ref):
+        return jnp.concatenate([ref[i] for i in range(TILE[w])] + [jnp.zeros((8 - TILE[w], LANES), F32)], axis=0)
+
     def merge1(w):
         cols = []
-        wait(r1l.at[w], r1l_r.at[w])
-        for k in KS:
-            ws, lse1[w, k] = _merge_weights([lrow[w, k]] + [r1l[w, k, x] for x in KS])
+        n = pl.ds(0, TILE[w])
+        wait(r1l.at[w, :, :, n], r1l_r.at[w])
+        for k in KS:
+            ws, l1 = _merge_weights([tile_of(w, r) for r in [lrow.at[w, k]] + [r1l.at[w, k, x] for x in KS]])
+            for i in range(TILE[w]):
+                lse1[w, k, i] = l1[i:i + 1]
             cols.append(columns(ws, k, ac[ORDERS[k][2]] * 32, 32))
         for k in KS:
             for o in RING_OFFS:
-                send(lse1.at[w, k], r2l.at[w, k, o - 1], r2l_s, r2l_r.at[w], ring(ORDERS[k][1], o))
+                send(lse1.at[w, k, n], r2l.at[w, k, o - 1, n], r2l_s.at[w], r2l_r.at[w], ring(ORDERS[k][1], o))
         wait(obuf.at[pl.ds(0, 12 * count(w))], r1_r.at[w])
         for k in KS:
             _, a2, a3 = ORDERS[k]
@@ -299,10 +308,10 @@
 
     def merge2(w):
         cols = []
-        wait(r2l.at[w], r2l_r.at[w])
+        wait(r2l.at[w, :, :, pl.ds(0, TILE[w])], r2l_r.at[w])
         for k in KS:
             _, a2, a3 = ORDERS[k]
-            ws, l2 = _merge_weights([lse1[w, k]] + [r2l[w, k, x] for x in KS])
+            ws, l2 = _merge_weights([tile_of(w, r) for r in [lse1.at[w, k]] + [r2l.at[w, k, x] for x in KS]])
             g = ac[a3] * 4 + ac[a2]
             lt = pltpu.roll(l2, ((16 - g) % 16) * 8, 1)
             s3l[w, k] = jnp.concatenate([lt] * 16, axis=0).T[0:8].reshape(8, 1, LANES)
@@ -319,17 +328,18 @@
             its = members(w, k)
             ys = [weighted(cols[k], i - its[0], [r1m[k, ac[ORDERS[k][1]], i]] + [r2d[k, x, i] for x in KS]) for i in its]
             n = len(its)
-            pm = _perm(64, 8 * n, lambda r, c: (c == (r % 8) * 8 + r // 8) & (r % 8 < n))
+            t = TILE[w]
+            pm = _perm(8 * t, 8 * n, lambda r, c: (c == (r % t) * 8 + r // t) & (r % t < n))
             tiles.append(jnp.dot(pm, jnp.concatenate(ys, axis=0).astype(BF16), preferred_element_type=F32))
         for k in KS:
-            s3src[w, k] = tiles[k].astype(BF16).reshape(8, 8, LAT)
+            t, s3, r3 = TILE[w], (s3a, s3b)[w], (r3a, r3b)[w]
             j0 = place(k)
+            for j in range(8):
+                s3[k, j] = tiles[k][t * j:t * j + t].astype(BF16)
             for off in (3, 4, 5, 2, 6, 1, 7):
                 j = (j0 + off) % 8
-                send(s3src.at[w, k, j], r3d.at[w, k, j0], r3_s, r3_r.at[w], line(ORDERS[k][0], j))
-            r3d[w, k, j0] = s3src[w, k, j0]
-
-    rows = {}
+                send(s3.at[k, j], r3.at[k, j0], r3_s.at[w], r3_r.at[w], line(ORDERS[k][0], j))
+            r3[k, j0] = s3[k, j0]
 
     def merge3(w):
         cols = []
@@ -340,11 +350,12 @@
             for h in DIRS:
                 ws[h::2], _ = _merge_weights(ls[h::2])
             cols.append(jnp.concatenate(ws, axis=0).T[0:8])
-        wait(r3d.at[w, :, pl.ds(0, 7)], r3_r.at[w])
+        t, r3 = TILE[w], (r3a, r3b)[w]
+        wait(r3.at[:, pl.ds(0, 7)], r3_r.at[w])
         for k in KS:
             for h in DIRS:
-                ts = [r3d[w, k, j].astype(F32) * cols[k][:, j:j + 1] for j in range(h, 8, 2)]
-                rows[w, h, k] = functools.reduce(jnp.add, ts)
+                ts = [r3[k, j].astype(F32) * cols[k][:t, j:j + 1] for j in range(h, 8, 2)]
+                fin[w, h, k, :t] = functools.reduce(jnp.add, ts)
 
     merge1(0)
     merge1(1)
@@ -358,11 +369,13 @@
     merge2(1)
     merge3(0)
     wait(obuf.at[pl.ds(0, 192)], r1_s)
-    wait(r1l, r1l_s)
+    for w in DIRS:
+        n = pl.ds(0, TILE[w])
+        wait(r1l.at[w, :, :, n], r1l_s.at[w])
+        wait(r2l.at[w, :, :, n], r2l_s.at[w])
     wait(obuf.at[pl.ds(0, 48)], r2_s)
-    wait(r2l, r2l_s)
     merge3(1)
-    flat = jnp.concatenate([rows[w, h, k] for w in DIRS for h in DIRS for k in KS], axis=0).astype(BF16)
+    flat = fin[...].reshape(96, LAT).astype(BF16)
 
     def pick(r, c):
         w, h, k, i = c // 48, (c // 24) % 2, (c // 8) % 3, c % 8
@@ -371,7 +384,8 @@
 
     o_ref[...] = jnp.dot(_perm(32, 96, pick), flat, preferred_element_type=F32).astype(BF16)
 
-    wait(r3d.at[:, :, pl.ds(0, 7)], r3_s)
+    wait(r3a.at[:, pl.ds(0, 7)], r3_s.at[0])
+    wait(r3b.at[:, pl.ds(0, 7)], r3_s.at[1])
     wait(r3l.at[:, :, pl.ds(0, 7)], r3l_s)
 
 
@@ -380,17 +394,19 @@
         dma = pltpu.SemaphoreType.DMA
         V = pltpu.VMEM
         anyspace = pl.BlockSpec(memory_space=pl.ANY)
-        tile, qtile, row = (8, LAT), (8, QW), (8, LANES)
+        tile, qtile = (8, LAT), (8, QW)
         line = (2, 3, 8)
         scratch = [
             pltpu.SMEM((32,), jnp.int32), V((32, QW), BF16), V((2, 3) + qtile, BF16), V((3, 8) + qtile, BF16),
             V((144, 8, LAT + LANES), BF16), V((144,) + tile, BF16),
-            V((16, 64) + qtile, BF16), V((288,) + tile, BF16), V((2, 3) + row, F32), V((3, LANES, LANES), F32),
-            V((3, NI, 3, 4) + tile, BF16), V((2, 3, 3) + row, F32), V((3, 4, NI) + tile, BF16), V((2, 3) + row, F32),
-            V((3, 3, NI) + tile, BF16), V((2, 3, 3) + row, F32),
-            V(line + tile, BF16), V(line + (1, LANES), F32), V(line + tile, BF16), V(line + (1, LANES), F32),
+            V((16, 64) + qtile, BF16), V((288,) + tile, BF16), V((2, 3, SPLIT, 1, LANES), F32), V((3, LANES, LANES), F32),
+            V((3, NI, 3, 4) + tile, BF16), V((2, 3, 3, SPLIT, 1, LANES), F32), V((3, 4, NI) + tile, BF16), V((2, 3, SPLIT, 1, LANES), F32),
+            V((3, 3, NI) + tile, BF16), V((2, 3, 3, SPLIT, 1, LANES), F32),
+            V((3, 8, TILE[0], LAT), BF16), V((3, 8, TILE[1], LAT), BF16), V(line + (1, LANES), F32),
+            V((3, 8, TILE[0], LAT), BF16), V((3, 8, TILE[1], LAT), BF16), V(line + (1, LANES), F32),
+            V((2, 2, 3) + tile, F32),
             dma, dma, dma, dma, dma, dma, dma((2,)), dma((NI,)), dma((2,)), dma((NI,)), dma((NI,)),
-            dma, dma((2,)), dma, dma((2,)), dma, dma((2,)), dma, dma((2,)), dma, dma((2,)), dma, dma((2,)),
+            dma, dma((2,)), dma((2,)), dma((2,)), dma, dma((2,)), dma((2,)), dma((2,)), dma((2,)), dma((2,)), dma, dma((2,)),
         ]
         o = pl.pallas_call(
             _kernel,

time: 42.9 us -> 42.5 us (level)
  no operation moved by 1% of the time
where the time goes in v8:
time: 42.5 us; the launch traced here: 42.4 us
  Pallas kernels  41.8 us (98%)
  local copies, waits for them, and re-layouts  0.62 us (1%)
    pallas_call x1, Pallas kernels, local(): pl.pallas_call(_kernel, out_shape=V((32, LAT), BF16), in_specs=[anyspace]...  41.8 us

profile of v8, /device:TPU:1, one launch (start us, length us, event | category | flops | bytes accessed | tf_op | source)
XLA Modules:
  0.0 42.4 jit_solution(17463935204685446777)
XLA Ops:
  0.0 41.8 %shard_map.37 = bf16[32,512]{1,0:T(8,128)(2,1)S(1)} custom-call(s32[32]{0:T(128)} %lens_h.1, bf16[32,576]{1,0:T(8,128)(2,1)} %bitcast.5, bf16[32,32,8,576]{3,2,1,0:T(8,128)(2,1)} %bitcast.4), custom_call_target="tpu_custom_call" | custom-call | tf_op jit(solution)/shard_map/pallas_call | solution.py:411
  41.8 0.6 %copy.5 = bf16[32,1,512]{2,0,1:T(8,128)(2,1)} copy(bf16[32,1,512]{2,0,1:T(8,128)(2,1)S(1)} %bitcast.3) | data formatting | bytes 65536

commit v9 on v8

--- a/solution.py
+++ b/solution.py
@@ -18,11 +18,12 @@
 
 STRIDE = (2, 8, 32)
 ORDERS = ((0, 1, 2), (1, 2, 0), (2, 0, 1))
-COUNT = (6, 5, 5)
+BASE = 15
+COUNT = (6, 6, 5)
 NI = 6
 SPLIT = 4
 TILE = (SPLIT, NI - SPLIT)
-ORDER, RELAYED = (0, 3, 4, 5, 1, 2), (3, 4, 5)
+ORDER, RELAYED = (0, 4, 5, 1, 2, 3), (4, 5)
 
 
 LAT, QW, LANES = 512, 576, 128
@@ -71,12 +72,22 @@
         pltpu.make_async_copy(ref, ref, sem).wait()
 
     def ks_of(i):
-        return KS if i < NI - 1 else range(1)
+        return KS if i < NI - 1 else DIRS
+
+    def only(i, f):
+        if i < NI - 1:
+            f()
+        else:
+            pl.when(core == 1)(f)
+
+    def by_core(f):
+        for c in DIRS:
+            pl.when(core == c)(functools.partial(f, c))
 
     bar = pltpu.get_barrier_semaphore()
     pl.semaphore_signal(bar, inc=1, device_id=partner, device_id_type=MESH)
-    for a in KS:
-        for off in RING_OFFS:
+    for off in (2, 1, 3):
+        for a in KS:
             for c2 in DIRS:
                 peer = d + ((co[a] + off) % 4 - co[a]) * STRIDE[a] + c2 - core
                 pl.semaphore_signal(bar, inc=1, device_id={'dcp': peer}, device_id_type=MESH)
@@ -87,19 +98,29 @@
 
     def cache_rows(i, half):
         n = len(ks_of(i))
-        return c_h.at[pl.ds(16 * half + 3 * i, n)], cbuf.at[pl.ds(3 * i, n), pl.ds(32 * core, 32)]
-
-    for i in range(NI):
-        src, dst = cache_rows(i, core)
+        return c_h.at[pl.ds(BASE * half + 3 * i, n)], cbuf.at[pl.ds(3 * i, n), pl.ds(32 * core, 32)]
+
+    def load_rows(i, half):
+        src, dst = cache_rows(i, half)
         pltpu.make_async_copy(src, dst, c_r).start()
+
+    for i in range(NI - 1):
+        load_rows(i, core)
+    pl.when(core == 1)(lambda: load_rows(NI - 1, 1))
 
     lrow[...] = jnp.zeros_like(lrow)
     fin[...] = jnp.zeros_like(fin)
+
+    @pl.when(core == 0)
+    def _():
+        for k in DIRS:
+            obuf[pl.ds((k * NI + NI - 1) * 16, 16)] = jnp.zeros((16, 8, LAT), BF16)
+            r1d[k, NI - 1] = jnp.zeros((3, 4, 8, LAT), BF16)
     load_l.wait()
 
     def sel(r, c):
         s = 3 * (r % 8) + (r // 8) % 3
-        return (c == 16 * (r // 24) + s) & (s < 16)
+        return (c == BASE * (r // 24) + s) & (s < BASE + 2 * (r // 24))
 
     load_q.wait()
     qp = jnp.dot(_perm(48, 32, sel), q_in[...], preferred_element_type=F32).astype(BF16)
@@ -120,9 +141,14 @@
             peer = {'dcp': d + ((oc + off) % 4 - oc) * ost + 1 - 2 * core}
             send(s1src.at[1 - core, k], s1buf.at[k, oc * 2 + core], s1_s, s1_r, peer)
         s1buf[k, j0] = s1src[core, k]
-    for i in range(NI):
-        src, dst = cache_rows(i, 1 - core)
+
+    def push_rows(i, half):
+        src, dst = cache_rows(i, half)
         send(src, dst, c_s, c_r, partner)
+
+    for i in range(NI - 1):
+        push_rows(i, 1 - core)
+    pl.when(core == 0)(lambda: push_rows(NI - 1, 1))
 
     def q_of(i):
         return q_odd if i % 2 else q_even
@@ -161,9 +187,12 @@
             if i % 2 == 0:
                 y = jnp.concatenate([y, rows[8 * i + 8:8 * i + 16, LAT:]], axis=1)
             q_of(i)[q_slot(k, i) + ac[a3] * 4 + ac[a2]] = y.astype(BF16)
-    for i in ORDER:
+    def rows2(i):
         for k in ks_of(i):
             stage2(k, i)
+
+    for i in ORDER:
+        only(i, functools.partial(rows2, i))
 
     def stage3(i):
         n = len(ks_of(i))
@@ -184,11 +213,11 @@
     def arrive(i):
         n = len(ks_of(i))
         if i == 0:
-            wait(cbuf, c_r)
+            by_core(lambda c: wait(cbuf.at[pl.ds(0, BASE + 2 * c)], c_r))
         wait(q_of(i).at[pl.ds(0, (8 if i in RELAYED else 12) * n)], s3_r.at[i])
 
     for i in ORDER:
-        stage3(i)
+        only(i, functools.partial(stage3, i))
 
     chip8 = (d // 2) * 16
 
@@ -209,7 +238,7 @@
         return (st + lax.dot_general(cs[:, LAT:], rope, dims, preferred_element_type=F32)) * SCALE2
 
     def softmax(st, k, i):
-        ok = pos < lens[16 * core + 3 * i + k] - chip8
+        ok = pos < lens[BASE * core + 3 * i + k] - chip8
         st = jnp.where(ok, st, NEG)
         m = jnp.max(st, axis=0, keepdims=True)
         has = m > NEG
@@ -230,9 +259,9 @@
     def wave(i):
         return 0 if i < SPLIT else 1
 
-    def send1(k, i):
-        a3 = ORDERS[k][2]
-        for o in (2, 1, 3):
+    def send1(batch):
+        for o, (k, i) in [(o, x) for o in (2, 1, 3) for x in batch]:
+            a3 = ORDERS[k][2]
             b = obuf.at[pl.ds(slot(k, i) + ((ac[a3] + o) % 4) * 4, 4)]
             send(b, r1d.at[k, i, o - 1], r1_s, r1_r.at[wave(i)], ring(a3, o))
 
@@ -248,25 +277,30 @@
                 n = pl.ds(0, TILE[w])
                 send(lrow.at[w, k, n], r1l.at[w, k, o - 1, n], r1l_s.at[w], r1l_r.at[w], ring(ORDERS[k][2], o))
 
-    for i in range(NI - 1):
+    for i in range(NI - 2):
         batch = [(k, i) for k in KS]
         with jax.named_scope(f"arrive{i}"):
             arrive(i)
-            if i == NI - 2:
-                arrive(i + 1)
-                batch.append((0, i + 1))
         with jax.named_scope(f"attend{i}"):
             attend(batch)
         with jax.named_scope(f"rest{i}"):
             if i == 0:
                 for x in RELAYED:
-                    forward(x)
+                    only(x, functools.partial(forward, x))
             if i == SPLIT - 1:
                 send1_lse(0)
-            if i == NI - 2:
-                send1_lse(1)
-            for k, x in batch:
-                send1(k, x)
+            send1(batch)
+
+
+    @by_core
+    def _(c):
+        last = range(NI - 2, NI - 1 + c)
+        for i in last:
+            arrive(i)
+        batch = [(k, i) for i in last for k in ks_of(i)]
+        attend(batch)
+        send1_lse(1)
+        send1(batch)
 
 
     def columns(ws, k, row, n):
@@ -292,7 +326,10 @@
         for k in KS:
             for o in RING_OFFS:
                 send(lse1.at[w, k, n], r2l.at[w, k, o - 1, n], r2l_s.at[w], r2l_r.at[w], ring(ORDERS[k][1], o))
-        wait(obuf.at[pl.ds(0, 12 * count(w))], r1_r.at[w])
+        if w == 0:
+            wait(obuf.at[pl.ds(0, 12 * count(w))], r1_r.at[w])
+        else:
+            by_core(lambda c: wait(obuf.at[pl.ds(0, 12 * (count(1) - 2 + 2 * c))], r1_r.at[w]))
         for k in KS:
             _, a2, a3 = ORDERS[k]
             its = members(w, k)
@@ -361,26 +398,30 @@
     merge1(1)
     merge2(0)
     wait(s1buf.at[:, pl.ds(0, 7)], s1_s)
-    wait(cbuf.at[pl.ds(0, 8)], c_s)
-    for par in DIRS:
-        its = [i for i in range(NI) for _ in ks_of(i) if i % 2 == par]
-        wait(q_of(par).at[pl.ds(0, 3 * len(its))], s2_s.at[par])
-        wait(q_of(par).at[pl.ds(0, 12 * len(its))], s3_s.at[par])
+
+    @by_core
+    def _(c):
+        wait(cbuf.at[pl.ds(0, BASE + 2 * (1 - c)), pl.ds(0, 32)], c_s)
+        for par in DIRS:
+            its = [i for i in range(NI - 1 + c) for _ in ks_of(i) if i % 2 == par]
+            wait(q_of(par).at[pl.ds(0, 3 * len(its))], s2_s.at[par])
+            wait(q_of(par).at[pl.ds(0, 12 * len(its))], s3_s.at[par])
+
     merge2(1)
     merge3(0)
-    wait(obuf.at[pl.ds(0, 192)], r1_s)
+    by_core(lambda c: wait(obuf.at[pl.ds(0, 12 * (BASE + 2 * c))], r1_s))
     for w in DIRS:
         n = pl.ds(0, TILE[w])
         wait(r1l.at[w, :, :, n], r1l_s.at[w])
         wait(r2l.at[w, :, :, n], r2l_s.at[w])
-    wait(obuf.at[pl.ds(0, 48)], r2_s)
+    wait(obuf.at[pl.ds(0, 51)], r2_s)
     merge3(1)
     flat = fin[...].reshape(96, LAT).astype(BF16)
 
     def pick(r, c):
         w, h, k, i = c // 48, (c // 24) % 2, (c // 8) % 3, c % 8
         s = 3 * (i + w * SPLIT) + k
-        return (r == 16 * h + s) & (s < 16) & (i < SPLIT)
+        return (r == BASE * h + s) & (s < BASE + 2 * h) & (i < SPLIT)
 
     o_ref[...] = jnp.dot(_perm(32, 96, pick), flat, preferred_element_type=F32).astype(BF16)
 
@@ -399,7 +440,7 @@
         scratch = [
             pltpu.SMEM((32,), jnp.int32), V((32, QW), BF16), V((2, 3) + qtile, BF16), V((3, 8) + qtile, BF16),
             V((144, 8, LAT + LANES), BF16), V((144,) + tile, BF16),
-            V((16, 64) + qtile, BF16), V((288,) + tile, BF16), V((2, 3, SPLIT, 1, LANES), F32), V((3, LANES, LANES), F32),
+            V((BASE + 2, 64) + qtile, BF16), V((288,) + tile, BF16), V((2, 3, SPLIT, 1, LANES), F32), V((3, LANES, LANES), F32),
             V((3, NI, 3, 4) + tile, BF16), V((2, 3, 3, SPLIT, 1, LANES), F32), V((3, 4, NI) + tile, BF16), V((2, 3, SPLIT, 1, LANES), F32),
             V((3, 3, NI) + tile, BF16), V((2, 3, 3, SPLIT, 1, LANES), F32),
             V((3, 8, TILE[0], LAT), BF16), V((3, 8, TILE[1], LAT), BF16), V(line + (1, LANES), F32),

time: 42.5 us -> 42 us (0.988)
  Pallas kernels: 41.8 us -> 41.3 us
    pallas_call x1, Pallas kernels: 41.8 us -> 41.3 us  [local(): pl.pallas_call(_kernel, out_shape=V((32, LAT), BF16), in_specs=[anyspace]...]
where the time goes in v9:
time: 42 us; the launch traced here: 41.9 us
  Pallas kernels  41.3 us (98%)
  local copies, waits for them, and re-layouts  0.62 us (1%)
    pallas_call x1, Pallas kernels, local(): pl.pallas_call(_kernel, out_shape=V((32, LAT), BF16), in_specs=[anyspace]...  41.3 us

profile of v9, /device:TPU:1, one launch (start us, length us, event | category | flops | bytes accessed | tf_op | source)
XLA Modules:
  0.0 41.9 jit_solution(3147470759872059719)
XLA Ops:
  0.0 41.3 %shard_map.37 = bf16[32,512]{1,0:T(8,128)(2,1)S(1)} custom-call(s32[32]{0:T(128)} %lens_h.1, bf16[32,576]{1,0:T(8,128)(2,1)} %bitcast.5, bf16[32,32,8,576]{3,2,1,0:T(8,128)(2,1)} %bitcast.4), custom_call_target="tpu_custom_call" | custom-call | tf_op jit(solution)/shard_map/pallas_call | solution.py:452
  41.3 0.6 %copy.5 = bf16[32,1,512]{2,0,1:T(8,128)(2,1)} copy(bf16[32,1,512]{2,0,1:T(8,128)(2,1)S(1)} %bitcast.3) | data formatting | bytes 65536

commit v10 on v9

--- a/solution.py
+++ b/solution.py
@@ -45,7 +45,7 @@
 
 
 def _kernel(lens_h, q_h, c_h, o_ref,
-            lens, q_in, s1src, s1buf, q_even, q_odd, cbuf, obuf, lrow, wcol, r1d, r1l, r1m, lse1,
+            lens, q_in, s1a, s1b, b1a, b1b, q_even, q_odd, cbuf, obuf, lrow, wcol, r1d, r1l, r1m, lse1,
             r2d, r2l, s3a, s3b, s3l, r3a, r3b, r3l, fin,
             sem_l, sem_q, c_s, c_r, s1_s, s1_r, s2_s, s2_r, s3_s, s3_r, sf_r,
             r1_s, r1_r, r1l_s, r1l_r, r2_s, r2_r, r2l_s, r2l_r, r3_s, r3_r, r3l_s, r3l_r):
@@ -123,24 +123,29 @@
         return (c == BASE * (r // 24) + s) & (s < BASE + 2 * (r // 24))
 
     load_q.wait()
-    qp = jnp.dot(_perm(48, 32, sel), q_in[...], preferred_element_type=F32).astype(BF16)
-    s1src[...] = qp.reshape(2, 3, 8, QW)
+    qp = jnp.dot(_perm(48, 32, sel), q_in[...], preferred_element_type=F32)
+    for c in DIRS:
+        for k in KS:
+            r = 8 * (3 * c + k)
+            s1a[c, k] = qp[r:r + 2].astype(BF16)
+            s1b[c, k] = qp[r + 2:r + 6].astype(BF16)
     pl.semaphore_wait(bar, 19)
 
     def place(k):
         return ac[ORDERS[k][0]] * 2 + core
 
-    for k in KS:
-        n = ORDERS[k][0]
-        j0 = place(k)
-        oc = co[n] + co[nxt[n]] - ac[n]
-        ost = STRIDE[n] + STRIDE[nxt[n]] - stride[n]
-        for off in (2, 1, 3):
-            send(s1src.at[core, k], s1buf.at[k, j0], s1_s, s1_r, ring(n, off))
-        for off in (2, 1, 3, 0):
-            peer = {'dcp': d + ((oc + off) % 4 - oc) * ost + 1 - 2 * core}
-            send(s1src.at[1 - core, k], s1buf.at[k, oc * 2 + core], s1_s, s1_r, peer)
-        s1buf[k, j0] = s1src[core, k]
+    for part, (src, dst) in enumerate(((s1a, b1a), (s1b, b1b))):
+        for k in KS:
+            n = ORDERS[k][0]
+            j0 = place(k)
+            oc = co[n] + co[nxt[n]] - ac[n]
+            ost = STRIDE[n] + STRIDE[nxt[n]] - stride[n]
+            for off in (2, 1, 3):
+                send(src.at[core, k], dst.at[k, j0], s1_s.at[part], s1_r.at[part], ring(n, off))
+            for off in (2, 1, 3, 0):
+                peer = {'dcp': d + ((oc + off) % 4 - oc) * ost + 1 - 2 * core}
+                send(src.at[1 - core, k], dst.at[k, oc * 2 + core], s1_s.at[part], s1_r.at[part], peer)
+            dst[k, j0] = src[core, k]
 
     def push_rows(i, half):
         src, dst = cache_rows(i, half)
@@ -176,23 +181,31 @@
             send(b, b, s2_s.at[i % 2], s2_r.at[i], ring(ORDERS[k][1], off))
         copy3(k, i, 0)
 
-    tr = _perm(64, 64, lambda r, c: (r // 8 == c % 8) & (r % 8 == c // 8))
-    wait(s1buf.at[:, pl.ds(0, 7)], s1_r)
-    turned = [jnp.dot(tr, s1buf[k].reshape(64, QW), preferred_element_type=F32) for k in KS]
-    for k in KS:
-        rows = turned[k]
-        _, a2, a3 = ORDERS[k]
-        for i in range(COUNT[k]):
-            y = rows[8 * i:8 * i + 8, :LAT if i % 2 else QW]
-            if i % 2 == 0:
-                y = jnp.concatenate([y, rows[8 * i + 8:8 * i + 16, LAT:]], axis=1)
-            q_of(i)[q_slot(k, i) + ac[a3] * 4 + ac[a2]] = y.astype(BF16)
     def rows2(i):
         for k in ks_of(i):
             stage2(k, i)
 
+    def turn(buf, part, first, n):
+        wait(buf.at[:, pl.ds(0, 7)], s1_r.at[part])
+        tr = _perm(8 * n, 8 * n, lambda r, c: (r // 8 == c % n) & (r % 8 == c // n))
+        ins = [jnp.concatenate([buf[k, j].astype(F32) for j in range(8)], axis=0).astype(BF16) for k in KS]
+        outs = [jnp.dot(tr, v, preferred_element_type=F32) for v in ins]
+        for k in KS:
+            _, a2, a3 = ORDERS[k]
+            for i in range(first, min(first + n, COUNT[k])):
+                r = 8 * (i - first)
+                y = outs[k][r:r + 8, :LAT if i % 2 else QW]
+                if i % 2 == 0:
+                    y = jnp.concatenate([y, outs[k][r + 8:r + 16, LAT:]], axis=1)
+                q_of(i)[q_slot(k, i) + ac[a3] * 4 + ac[a2]] = y.astype(BF16)
+
+    turn(b1a, 0, 0, 2)
+    for i in range(2):
+        rows2(i)
+    turn(b1b, 1, 2, 4)
     for i in ORDER:
-        only(i, functools.partial(rows2, i))
+        if i > 1:
+            only(i, functools.partial(rows2, i))
 
     def stage3(i):
         n = len(ks_of(i))
@@ -397,7 +410,8 @@
     merge1(0)
     merge1(1)
     merge2(0)
-    wait(s1buf.at[:, pl.ds(0, 7)], s1_s)
+    wait(b1a.at[:, pl.ds(0, 7)], s1_s.at[0])
+    wait(b1b.at[:, pl.ds(0, 7)], s1_s.at[1])
 
     @by_core
     def _(c):
@@ -438,7 +452,7 @@
         tile, qtile = (8, LAT), (8, QW)
         line = (2, 3, 8)
         scratch = [
-            pltpu.SMEM((32,), jnp.int32), V((32, QW), BF16), V((2, 3) + qtile, BF16), V((3, 8) + qtile, BF16),
+            pltpu.SMEM((32,), jnp.int32), V((32, QW), BF16), V((2, 3, 2, QW), BF16), V((2, 3, 4, QW), BF16), V((3, 8, 2, QW), BF16), V((3, 8, 4, QW), BF16),
             V((144, 8, LAT + LANES), BF16), V((144,) + tile, BF16),
             V((BASE + 2, 64) + qtile, BF16), V((288,) + tile, BF16), V((2, 3, SPLIT, 1, LANES), F32), V((3, LANES, LANES), F32),
             V((3, NI, 3, 4) + tile, BF16), V((2, 3, 3, SPLIT, 1, LANES), F32), V((3, 4, NI) + tile, BF16), V((2, 3, SPLIT, 1, LANES), F32),
@@ -446,7 +460,7 @@
             V((3, 8, TILE[0], LAT), BF16), V((3, 8, TILE[1], LAT), BF16), V(line + (1, LANES), F32),
             V((3, 8, TILE[0], LAT), BF16), V((3, 8, TILE[1], LAT), BF16), V(line + (1, LANES), F32),
             V((2, 2, 3) + tile, F32),
-            dma, dma, dma, dma, dma, dma, dma((2,)), dma((NI,)), dma((2,)), dma((NI,)), dma((NI,)),
+            dma, dma, dma, dma, dma((2,)), dma((2,)), dma((2,)), dma((NI,)), dma((2,)), dma((NI,)), dma((NI,)),
             dma, dma((2,)), dma((2,)), dma((2,)), dma, dma((2,)), dma((2,)), dma((2,)), dma((2,)), dma((2,)), dma, dma((2,)),
         ]
         o = pl.pallas_call(

time: 42 us -> 41.9 us (level)
  no operation moved by 1% of the time
where the time goes in v10:
time: 41.9 us; the launch traced here: 41.8 us
  Pallas kernels  41.2 us (98%)
  local copies, waits for them, and re-layouts  0.62 us (1%)
    pallas_call x1, Pallas kernels, local(): pl.pallas_call(_kernel, out_shape=V((32, LAT), BF16), in_specs=[anyspace]...  41.2 us

profile of v10, /device:TPU:1, one launch (start us, length us, event | category | flops | bytes accessed | tf_op | source)
XLA Modules:
  0.0 41.8 jit_solution(4782201715058148004)
XLA Ops:
  0.0 41.2 %shard_map.37 = bf16[32,512]{1,0:T(8,128)(2,1)S(1)} custom-call(s32[32]{0:T(128)} %lens_h.1, bf16[32,576]{1,0:T(8,128)(2,1)} %bitcast.5, bf16[32,32,8,576]{3,2,1,0:T(8,128)(2,1)} %bitcast.4), custom_call_target="tpu_custom_call" | custom-call | tf_op jit(solution)/shard_map/pallas_call | solution.py:466
  41.2 0.6 %copy.5 = bf16[32,1,512]{2,0,1:T(8,128)(2,1)} copy(bf16[32,1,512]{2,0,1:T(8,128)(2,1)S(1)} %bitcast.3) | data formatting | bytes 65536

commit v11 on v10

--- a/solution.py
+++ b/solution.py
@@ -23,7 +23,7 @@
 NI = 6
 SPLIT = 4
 TILE = (SPLIT, NI - SPLIT)
-ORDER, RELAYED = (0, 4, 5, 1, 2, 3), (4, 5)
+ORDER, RELAYED = (0, 5, 4, 1, 2, 3), (5, 4)
 
 
 LAT, QW, LANES = 512, 576, 128
@@ -173,7 +173,7 @@
         a3 = ORDERS[k][2]
         for o in (1, 3) if i in RELAYED else (2, 1, 3):
             onward = i in RELAYED and off // 2 == o // 2
-            send(b, b, s3_s.at[i % 2], sf_r.at[i] if onward else s3_r.at[i], ring(a3, o))
+            send(b, b, s3_s.at[i % 2], sf_r.at[i - NI + 2] if onward else s3_r.at[i], ring(a3, o))
 
     def stage2(k, i):
         b = blk(k, i, 0)
@@ -215,7 +215,7 @@
                 copy3(k, i, off)
 
     def forward(i):
-        wait(q_of(i).at[pl.ds(0, 4 * len(ks_of(i)))], sf_r.at[i])
+        wait(q_of(i).at[pl.ds(0, 4 * len(ks_of(i)))], sf_r.at[i - NI + 2])
         for off in RING:
             for k in ks_of(i):
                 _, a2, a3 = ORDERS[k]
@@ -460,7 +460,7 @@
             V((3, 8, TILE[0], LAT), BF16), V((3, 8, TILE[1], LAT), BF16), V(line + (1, LANES), F32),
             V((3, 8, TILE[0], LAT), BF16), V((3, 8, TILE[1], LAT), BF16), V(line + (1, LANES), F32),
             V((2, 2, 3) + tile, F32),
-            dma, dma, dma, dma, dma((2,)), dma((2,)), dma((2,)), dma((NI,)), dma((2,)), dma((NI,)), dma((NI,)),
+            dma, dma, dma, dma, dma((2,)), dma((2,)), dma((2,)), dma((NI,)), dma((2,)), dma((NI,)), dma((2,)),
             dma, dma((2,)), dma((2,)), dma((2,)), dma, dma((2,)), dma((2,)), dma((2,)), dma((2,)), dma((2,)), dma, dma((2,)),
         ]
         o = pl.pallas_call(

time: 41.9 us -> 41.8 us (level)
  no operation moved by 1% of the time
where the time goes in v11:
time: 41.8 us; the launch traced here: 41.7 us
  Pallas kernels  41.1 us (98%)
  local copies, waits for them, and re-layouts  0.62 us (1%)
    pallas_call x1, Pallas kernels, local(): pl.pallas_call(_kernel, out_shape=V((32, LAT), BF16), in_specs=[anyspace]...  41.1 us

profile of v11, /device:TPU:1, one launch (start us, length us, event | category | flops | bytes accessed | tf_op | source)
XLA Modules:
  0.0 41.7 jit_solution(212098178109305416)
XLA Ops:
  0.0 41.1 %shard_map.37 = bf16[32,512]{1,0:T(8,128)(2,1)S(1)} custom-call(s32[32]{0:T(128)} %lens_h.1, bf16[32,576]{1,0:T(8,128)(2,1)} %bitcast.5, bf16[32,32,8,576]{3,2,1,0:T(8,128)(2,1)} %bitcast.4), custom_call_target="tpu_custom_call" | custom-call | tf_op jit(solution)/shard_map/pallas_call | solution.py:466
  41.1 0.6 %copy.5 = bf16[32,1,512]{2,0,1:T(8,128)(2,1)} copy(bf16[32,1,512]{2,0,1:T(8,128)(2,1)S(1)} %bitcast.3) | data formatting | bytes 65536

commit v12 on v11

--- a/solution.py
+++ b/solution.py
@@ -140,11 +140,11 @@
             j0 = place(k)
             oc = co[n] + co[nxt[n]] - ac[n]
             ost = STRIDE[n] + STRIDE[nxt[n]] - stride[n]
-            for off in (2, 1, 3):
-                send(src.at[core, k], dst.at[k, j0], s1_s.at[part], s1_r.at[part], ring(n, off))
             for off in (2, 1, 3, 0):
                 peer = {'dcp': d + ((oc + off) % 4 - oc) * ost + 1 - 2 * core}
                 send(src.at[1 - core, k], dst.at[k, oc * 2 + core], s1_s.at[part], s1_r.at[part], peer)
+            for off in (2, 1, 3):
+                send(src.at[core, k], dst.at[k, j0], s1_s.at[part], s1_r.at[part], ring(n, off))
             dst[k, j0] = src[core, k]
 
     def push_rows(i, half):
@@ -186,8 +186,8 @@
             stage2(k, i)
 
     def turn(buf, part, first, n):
+        tr = _perm(8 * n, 8 * n, lambda r, c: (r // 8 == c % n) & (r % 8 == c // n))
         wait(buf.at[:, pl.ds(0, 7)], s1_r.at[part])
-        tr = _perm(8 * n, 8 * n, lambda r, c: (r // 8 == c % n) & (r % 8 == c // n))
         ins = [jnp.concatenate([buf[k, j].astype(F32) for j in range(8)], axis=0).astype(BF16) for k in KS]
         outs = [jnp.dot(tr, v, preferred_element_type=F32) for v in ins]
         for k in KS:
@@ -372,15 +372,16 @@
                 j = (j0 + off) % 8
                 send(s3l.at[w, k, j], r3l.at[w, k, j0], r3l_s, r3l_r.at[w], line(ORDERS[k][0], j))
             r3l[w, k, j0] = s3l[w, k, j0]
+        t = TILE[w]
+        pms = {n: _perm(8 * t, 8 * n, lambda r, c: (c == (r % t) * 8 + r // t) & (r % t < n))
+               for n in sorted({len(members(w, k)) for k in KS})}
         wait(obuf.at[pl.ds(0, 3 * count(w))], r2_r.at[w])
         tiles = []
         for k in KS:
             its = members(w, k)
             ys = [weighted(cols[k], i - its[0], [r1m[k, ac[ORDERS[k][1]], i]] + [r2d[k, x, i] for x in KS]) for i in its]
             n = len(its)
-            t = TILE[w]
-            pm = _perm(8 * t, 8 * n, lambda r, c: (c == (r % t) * 8 + r // t) & (r % t < n))
-            tiles.append(jnp.dot(pm, jnp.concatenate(ys, axis=0).astype(BF16), preferred_element_type=F32))
+            tiles.append(jnp.dot(pms[n], jnp.concatenate(ys, axis=0).astype(BF16), preferred_element_type=F32))
         for k in KS:
             t, s3, r3 = TILE[w], (s3a, s3b)[w], (r3a, r3b)[w]
             j0 = place(k)
@@ -429,15 +430,16 @@
         wait(r1l.at[w, :, :, n], r1l_s.at[w])
         wait(r2l.at[w, :, :, n], r2l_s.at[w])
     wait(obuf.at[pl.ds(0, 51)], r2_s)
-    merge3(1)
-    flat = fin[...].reshape(96, LAT).astype(BF16)
-
     def pick(r, c):
         w, h, k, i = c // 48, (c // 24) % 2, (c // 8) % 3, c % 8
         s = 3 * (i + w * SPLIT) + k
         return (r == BASE * h + s) & (s < BASE + 2 * h) & (i < SPLIT)
 
-    o_ref[...] = jnp.dot(_perm(32, 96, pick), flat, preferred_element_type=F32).astype(BF16)
+    pm = _perm(32, 96, pick)
+    merge3(1)
+    flat = fin[...].reshape(96, LAT).astype(BF16)
+
+    o_ref[...] = jnp.dot(pm, flat, preferred_element_type=F32).astype(BF16)
 
     wait(r3a.at[:, pl.ds(0, 7)], r3_s.at[0])
     wait(r3b.at[:, pl.ds(0, 7)], r3_s.at[1])

time: 41.8 us -> 41.9 us (level)
  no operation moved by 1% of the time
where the time goes in v12:
time: 41.9 us; the launch traced here: 41.8 us
  Pallas kernels  41.1 us (98%)
  local copies, waits for them, and re-layouts  0.62 us (1%)
    pallas_call x1, Pallas kernels, local(): pl.pallas_call(_kernel, out_shape=V((32, LAT), BF16), in_specs=[anyspace]...  41.1 us

profile of v12, /device:TPU:1, one launch (start us, length us, event | category | flops | bytes accessed | tf_op | source)
XLA Modules:
  0.0 41.8 jit_solution(5593948726099923563)
XLA Ops:
  0.0 41.1 %shard_map.37 = bf16[32,512]{1,0:T(8,128)(2,1)S(1)} custom-call(s32[32]{0:T(128)} %lens_h.1, bf16[32,576]{1,0:T(8,128)(2,1)} %bitcast.5, bf16[32,32,8,576]{3,2,1,0:T(8,128)(2,1)} %bitcast.4), custom_call_target="tpu_custom_call" | custom-call | tf_op jit(solution)/shard_map/pallas_call | solution.py:468
  41.2 0.6 %copy.5 = bf16[32,1,512]{2,0,1:T(8,128)(2,1)} copy(bf16[32,1,512]{2,0,1:T(8,128)(2,1)S(1)} %bitcast.3) | data formatting | bytes 65536

commit v13 on v12

--- a/solution.py
+++ b/solution.py
@@ -140,11 +140,11 @@
             j0 = place(k)
             oc = co[n] + co[nxt[n]] - ac[n]
             ost = STRIDE[n] + STRIDE[nxt[n]] - stride[n]
+            for off in (2, 1, 3):
+                send(src.at[core, k], dst.at[k, j0], s1_s.at[part], s1_r.at[part], ring(n, off))
             for off in (2, 1, 3, 0):
                 peer = {'dcp': d + ((oc + off) % 4 - oc) * ost + 1 - 2 * core}
                 send(src.at[1 - core, k], dst.at[k, oc * 2 + core], s1_s.at[part], s1_r.at[part], peer)
-            for off in (2, 1, 3):
-                send(src.at[core, k], dst.at[k, j0], s1_s.at[part], s1_r.at[part], ring(n, off))
             dst[k, j0] = src[core, k]
 
     def push_rows(i, half):

time: 41.9 us -> 41.8 us (level)
  no operation moved by 1% of the time
where the time goes in v13:
time: 41.8 us; the launch traced here: 41.7 us
  Pallas kernels  41.1 us (98%)
  local copies, waits for them, and re-layouts  0.62 us (1%)
    pallas_call x1, Pallas kernels, local(): pl.pallas_call(_kernel, out_shape=V((32, LAT), BF16), in_specs=[anyspace]...  41.1 us

profile of v13, /device:TPU:1, one launch (start us, length us, event | category | flops | bytes accessed | tf_op | source)
XLA Modules:
  0.0 41.7 jit_solution(4728695567593904463)
XLA Ops:
  0.0 41.1 %shard_map.37 = bf16[32,512]{1,0:T(8,128)(2,1)S(1)} custom-call(s32[32]{0:T(128)} %lens_h.1, bf16[32,576]{1,0:T(8,128)(2,1)} %bitcast.5, bf16[32,32,8,576]{3,2,1,0:T(8,128)(2,1)} %bitcast.4), custom_call_target="tpu_custom_call" | custom-call | tf_op jit(solution)/shard_map/pallas_call | solution.py:468
  41.1 0.6 %copy.5 = bf16[32,1,512]{2,0,1:T(8,128)(2,1)} copy(bf16[32,1,512]{2,0,1:T(8,128)(2,1)S(1)} %bitcast.3) | data formatting | bytes 65536
